TPU v7x, 128 devices: a whole 4x4x4 slice. The times are simulated.
128 devices in a mesh: row: 16 (over y, x_hi, core), col: 8 (over x_lo, z).
Axes of the slice: x: 4 (x_hi: 2, x_lo: 2; x = x_hi * 2 + x_lo), y: 4, z: 4, core: 2. Of those that a mesh axis runs over, the one named last changes fastest.
Arguments:
- sqrt_iterate: float32 [256, 128, 1024], P(('row', 'col'))
- inverse_iterate: float32 [256, 128, 1024], P(('row', 'col'))
- pattern: int32 [256, 8], replicated, may hold values from 0 to 255, as said below
- keep_mask: int32 [256, 8], replicated, may hold values 0 or 1
- row_order: int32 [256], replicated, may hold values from 0 to 255, as said below
Outputs:
- sqrt_next: float32 [256, 128, 1024], P(('row', 'col'))
- inverse_next: float32 [256, 128, 1024], P(('row', 'col'))
Inputs may be any that keep to these rules, and one draw needn't show every extreme that they name: row_order holds each of 0 to 255 once. pattern[s, 0] = row_order[s]; the labels of one row are distinct; each label in row s is that of a block row stored on the same device as s, on one of the two devices one step away along row (wrapping), or on the next device along col (wrapping). Stored position s lies on device index (s // 2) in the order of the mesh with row slowest.
All inputs are finite; a program needn't handle non-finite values.
Results may differ from a plain program's by a relative error of at most 0.00011.
Values sent between devices are 32-bit elements; how exact they have to be, the bound alone decides.
A program may use at most 128 MiB of HBM per device.

v0:
```python
import jax
import jax.numpy as jnp
from jax import lax
from jax.sharding import PartitionSpec as P

PRECISE = lax.Precision.HIGHEST


def with_halo(block, sides, width):
    for axis, dim in sides:
        count = lax.axis_size(axis)
        forward = [(i, i + 1) for i in range(count - 1)]
        forward.append((count - 1, 0))
        backward = [(target, source) for source, target in forward]
        low = lax.ppermute(
            lax.slice_in_dim(block, block.shape[dim] - width, None, axis=dim), axis, forward
        )
        high = lax.ppermute(lax.slice_in_dim(block, 0, width, axis=dim), axis, backward)
        block = jnp.concatenate([low, block, high], axis=dim)
    return block


def shifted(block, axis, distance):
    devices = range(lax.axis_size(axis))
    route = [((i - distance) % len(devices), i) for i in devices]
    return lax.ppermute(block, axis, route)


def extended_index(position, rows_dev, row_devices, col_devices, row_here, col_here):
    device = position // rows_dev
    offset = position % rows_dev
    row_of = device // col_devices
    col_of = device % col_devices
    same_col = col_of == col_here
    region = jnp.where(
        same_col & (row_of == row_here),
        1,
        jnp.where(
            same_col & (row_of == (row_here + row_devices - 1) % row_devices),
            0,
            jnp.where(same_col, 2, 3),
        ),
    )
    return region * rows_dev + offset


def filtered_product(left_factor, extended, ext_index, selector, kept_cols):
    rows_dev, block_size, row_width = left_factor.shape
    slot_count = row_width // block_size
    picked = extended[ext_index].reshape(rows_dev, slot_count, block_size, slot_count, block_size)
    chosen = jnp.einsum("skimj,skpm->skipj", picked, selector, precision=PRECISE)
    chosen = chosen.reshape(rows_dev, row_width, row_width)
    result = jnp.einsum(
        "sik,skn->sin", left_factor, chosen, precision=PRECISE, preferred_element_type=jnp.float32
    )
    return result * kept_cols


def local(sqrt_iterate, inverse_iterate, pattern, keep_mask, row_order):
    rows_dev, block_size, row_width = sqrt_iterate.shape
    slot_count = row_width // block_size
    row_devices = lax.axis_size("row")
    col_devices = lax.axis_size("col")
    row_here = lax.axis_index("row")
    col_here = lax.axis_index("col")
    block_rows = row_order.shape[0]
    inverse_order = (
        jnp.zeros((block_rows,), jnp.int32)
        .at[row_order]
        .set(jnp.arange(block_rows, dtype=jnp.int32))
    )
    first_row = (row_here * col_devices + col_here) * rows_dev
    local_pattern = lax.dynamic_slice_in_dim(pattern, first_row, rows_dev, 0)
    local_keep = lax.dynamic_slice_in_dim(keep_mask, first_row, rows_dev, 0)
    position = inverse_order[local_pattern]
    ext_index = extended_index(position, rows_dev, row_devices, col_devices, row_here, col_here)
    selector = (pattern[position][:, :, None, :] == local_pattern[:, None, :, None]).astype(
        jnp.float32
    )
    slot_ids = jnp.arange(slot_count, dtype=jnp.int32)
    kept = jnp.maximum(local_keep, (slot_ids == 0).astype(jnp.int32)[None, :])
    kept_cols = jnp.repeat(kept.astype(jnp.float32), block_size, axis=1)[:, None, :]
    identity = (jnp.arange(row_width)[None, :] == jnp.arange(block_size)[:, None]).astype(
        jnp.float32
    )
    cycle_sqrt = with_halo(sqrt_iterate, (("row", 0),), rows_dev)
    side_sqrt = shifted(sqrt_iterate, "col", -1)
    around_sqrt = jnp.concatenate([cycle_sqrt, side_sqrt], axis=0)
    product = filtered_product(inverse_iterate, around_sqrt, ext_index, selector, kept_cols)
    factor = 1.5 * identity[None] - 0.5 * product
    stacked = jnp.stack((factor, inverse_iterate))
    cycle_parts = with_halo(stacked, (("row", 1),), rows_dev)
    side_parts = shifted(stacked, "col", -1)
    around_pair = jnp.concatenate([cycle_parts, side_parts], axis=1)
    around_factor = around_pair[0]
    around_inverse = around_pair[1]
    sqrt_next = filtered_product(sqrt_iterate, around_factor, ext_index, selector, kept_cols)
    inverse_next = filtered_product(factor, around_inverse, ext_index, selector, kept_cols)
    return (sqrt_next, inverse_next)


def solution(mesh):
    in_specs = (P(("row", "col"), None, None), P(("row", "col"), None, None), P(), P(), P())
    out_specs = (P(("row", "col"), None, None), P(("row", "col"), None, None))
    return jax.shard_map(local, mesh=mesh, in_specs=in_specs, out_specs=out_specs, check_vma=False)
```

profile of v0, /device:TPU:0, one launch (start us, length us, event | category | flops | bytes accessed | tf_op | source)
XLA Modules:
  0.0 296.0 jit_solution(17963667064059996020)
XLA Ops:
  0.6 5.1 %collective-permute-start.2 = (f32[2,128,1024]{2,1,0:T(8,128)}, f32[2,128,1024]{2,1,0:T(8,128)S(1)}, u32[]{:S(2)}, u32[]{:S(2)}) collective-permute-start(f32[2,128,1024]{2,1,0:T(8,128)} %param.5), channel_id=1, source_target_pairs={{1,0},{2,1},{3,2},{4,3},{5,4},{6,5},{7,6},{0,7},{9,8},{10,9},{11,1... | collective-permute-start | bytes 3145736 | tf_op jit(solution)/shard_map/ppermute | solution.py:26
  5.7 4.3 %collective-permute-start.1 = (f32[2,128,1024]{2,1,0:T(8,128)}, f32[2,128,1024]{2,1,0:T(8,128)}, u32[]{:S(2)}, u32[]{:S(2)}) collective-permute-start(f32[2,128,1024]{2,1,0:T(8,128)} %param.5), channel_id=1, source_target_pairs={{8,0},{16,8},{24,16},{32,24},{40,32},{48,40},{56,48},{64,56},{72,6... | collective-permute-start | bytes 3145736 | tf_op jit(solution)/shard_map/ppermute | solution.py:18
  10.1 0.0 collective-permute-start
  10.1 0.8 copy.21
  10.9 0.8 compare_select_fusion
  11.7 0.1 copy.20
  11.8 0.1 reshape.233
  11.9 0.1 copy.24
  12.0 0.1 copy.26
  12.0 0.7 compare_select_fusion.2
  12.7 1.4 scatter_custom_fusion
  14.1 0.7 gather_fusion
  14.8 0.1 gather.18
  14.9 0.1 reshape.241
  15.0 0.1 reshape.249
  15.1 0.1 broadcast_bitcast_fusion
  15.2 1.5 copy.27
  16.7 0.6 gather_fusion.1
  17.3 0.8 fusion.4
  18.1 11.5 %collective-permute-done.2 = f32[2,128,1024]{2,1,0:T(8,128)S(1)} collective-permute-done((f32[2,128,1024]{2,1,0:T(8,128)}, f32[2,128,1024]{2,1,0:T(8,128)S(1)}, u32[]{:S(2)}, u32[]{:S(2)}) %collective-permute-start.2) | collective-permute-done | bytes 1048608 | tf_op jit(solution)/shard_map/ppermute | solution.py:26
  29.6 21.3 %collective-permute-done.1 = f32[2,128,1024]{2,1,0:T(8,128)} collective-permute-done((f32[2,128,1024]{2,1,0:T(8,128)}, f32[2,128,1024]{2,1,0:T(8,128)}, u32[]{:S(2)}, u32[]{:S(2)}) %collective-permute-start.1) | collective-permute-done | bytes 1048608 | tf_op jit(solution)/shard_map/ppermute | solution.py:18
  50.9 4.5 %collective-permute-done = f32[2,128,1024]{2,1,0:T(8,128)} collective-permute-done((f32[2,128,1024]{2,1,0:T(8,128)}, f32[2,128,1024]{2,1,0:T(8,128)}, u32[]{:S(2)}, u32[]{:S(2)}) %collective-permute-start) | collective-permute-done | bytes 1048608 | tf_op jit(solution)/shard_map/ppermute | solution.py:15
  55.4 4.3 %pad_maximum_fusion.1 = f32[8,128,1024]{2,1,0:T(8,128)} fusion(f32[2,128,1024]{2,1,0:T(8,128)S(1)} %collective-permute-done.2, f32[2,128,1024]{2,1,0:T(8,128)} %collective-permute-done.1, f32[2,128,1024]{2,1,0:T(8,128)} %param.5, f32[2,128,1024]{2,1,0:T(8,128)} %collective-permute-done), kind=kLoop, calls=%fused_computation.9 | loop fusion | flops 3145728 | bytes 8388608 | tf_op jit(solution)/shard_map/concatenate | solution.py:88
  59.8 6.5 %gather_fusion.2 = f32[16,128,1024]{2,1,0:T(8,128)} fusion(f32[8,128,1024]{2,1,0:T(8,128)} %pad_maximum_fusion.1, s32[1024]{0:T(1024)S(1)} %pad_clamp_fusion), kind=kCustom, calls=%fused_computation.2 | custom fusion | bytes 16777280 | tf_op jit(solution)/shard_map/gather | solution.py:50
  66.3 5.5 %copy.38 = f32[256,8,8,128]{3,2,1,0:T(8,128)S(1)} copy(f32[256,8,8,128]{3,1,2,0:T(8,128)} %bitcast.60) | data formatting | bytes 16777216
  71.7 6.5 %convolution_bitcast_fusion.2 = f32[2,8,128,8,128]{4,3,2,1,0:T(8,128)} fusion(f32[2,8,128,8,128]{4,3,2,1,0:T(8,128)S(1)} %bitcast.61, s32[2,8]{1,0:T(2,128)S(1)} %copy.24, s32[2,8,8]{2,1,0:T(8,128)S(1)} %bitcast.67), kind=kOutput, calls=%fused_computation.12 | convolution fusion | flops 201327616 | bytes 16777792 | tf_op jit(solution)/shard_map/skimj,skpm->skipj/dot_general | solution.py:51
  78.3 9.3 %reshape.226 = f32[2,1024,1024]{2,1,0:T(8,128)} reshape(f32[2,8,128,8,128]{4,3,2,1,0:T(8,128)} %convolution_bitcast_fusion.2) | data formatting | bytes 16777216 | tf_op jit(solution)/shard_map/reshape | solution.py:52
  87.6 15.6 %fusion.3 = f32[2,128,1024]{1,2,0:T(8,128)S(1)} fusion(f32[2,1024,1024]{2,1,0:T(8,128)} %reshape.226, f32[2,128,1024]{2,1,0:T(8,128)S(1)} %copy-done, f32[2,1024]{1,0:T(2,128)S(1)} %bitcast.70, f32[128,1024]{0,1:T(8,128)} %fusion.4), kind=kOutput, calls=%fused_computation.20 | convolution fusion | flops 3222011904 | bytes 11018240 | tf_op jit(solution)/shard_map/sik,skn->sin/dot_general | solution.py:53
  103.3 0.1 pad_maximum_fusion.2
  103.4 0.1 collective-permute-start.5
  103.5 1.1 collective-permute-start.4
  104.6 0.0 collective-permute-start.3
  104.6 45.2 %collective-permute-done.5 = f32[2,2,128,1024]{2,3,1,0:T(8,128)S(1)} collective-permute-done((f32[2,2,128,1024]{2,3,1,0:T(8,128)S(1)}, f32[2,2,128,1024]{2,3,1,0:T(8,128)S(1)}, u32[]{:S(2)}, u32[]{:S(2)}) %collective-permute-start.5) | collective-permute-done | bytes 2097184 | tf_op jit(solution)/shard_map/ppermute | solution.py:26
  149.9 42.7 %collective-permute-done.4 = f32[2,2,128,1024]{2,3,1,0:T(8,128)S(1)} collective-permute-done((f32[2,2,128,1024]{2,3,1,0:T(8,128)S(1)}, f32[2,2,128,1024]{2,3,1,0:T(8,128)S(1)}, u32[]{:S(2)}, u32[]{:S(2)}) %collective-permute-start.4) | collective-permute-done | bytes 2097184 | tf_op jit(solution)/shard_map/ppermute | solution.py:18
  192.6 3.0 %collective-permute-done.3 = f32[2,2,128,1024]{2,3,1,0:T(8,128)S(1)} collective-permute-done((f32[2,2,128,1024]{2,3,1,0:T(8,128)S(1)}, f32[2,2,128,1024]{2,3,1,0:T(8,128)S(1)}, u32[]{:S(2)}, u32[]{:S(2)}) %collective-permute-start.3) | collective-permute-done | bytes 2097184 | tf_op jit(solution)/shard_map/ppermute | solution.py:15
  195.6 1.2 pad_maximum_fusion
  196.8 3.8 %slice_bitcast_fusion = (f32[8,128,1024]{1,2,0:T(8,128)}, f32[8,128,1024]{1,2,0:T(8,128)}) fusion(f32[2,8,128,1024]{2,3,1,0:T(8,128)S(1)} %pad_maximum_fusion), kind=kLoop, calls=%fused_computation.7 | loop fusion | bytes 16777216 | tf_op jit(solution)/shard_map/squeeze | solution.py:96
  200.6 6.5 %gather_fusion.4 = f32[16,128,1024]{1,2,0:T(8,128)} fusion(f32[8,128,1024]{1,2,0:T(8,128)} %get-tuple-element.8, s32[1024]{0:T(1024)S(1)} %pad_clamp_fusion), kind=kCustom, calls=%fused_computation.4 | custom fusion | bytes 16777280 | tf_op jit(solution)/shard_map/gather | solution.py:50
  207.1 8.7 %copy.30 = f32[2,8,128,8,128]{4,3,2,1,0:T(8,128)} copy(f32[2,8,128,8,128]{2,4,3,1,0:T(8,128)} %bitcast.62) | data formatting | bytes 16777216 | tf_op jit(solution)/shard_map/reshape | solution.py:50
  215.8 10.5 %convolution_bitcast_fusion = f32[2,8,128,8,128]{4,3,2,1,0:T(8,128)} fusion(f32[2,8,128,8,128]{4,3,2,1,0:T(8,128)} %copy.30, s32[2,8]{1,0:T(2,128)S(1)} %copy.24, s32[2,8,8]{2,1,0:T(8,128)S(1)} %bitcast.68), kind=kOutput, calls=%fused_computation.10 | convolution fusion | flops 201327616 | bytes 16777792 | tf_op jit(solution)/shard_map/skimj,skpm->skipj/dot_general | solution.py:51
  226.3 9.2 %reshape.230 = f32[2,1024,1024]{2,1,0:T(8,128)} reshape(f32[2,8,128,8,128]{4,3,2,1,0:T(8,128)} %convolution_bitcast_fusion) | data formatting | bytes 16777216 | tf_op jit(solution)/shard_map/reshape | solution.py:52
  235.6 8.1 %convolution_multiply_fusion = f32[2,128,1024]{2,1,0:T(8,128)} fusion(f32[2,128,1024]{1,2,0:T(8,128)S(1)} %fusion.3, f32[2,1024,1024]{2,1,0:T(8,128)} %reshape.230, f32[2,1024]{1,0:T(2,128)S(1)} %bitcast.71), kind=kOutput, calls=%fused_computation.14 | convolution fusion | flops 3221487616 | bytes 10493952 | tf_op jit(solution)/shard_map/sik,skn->sin/dot_general | solution.py:53
  243.6 6.5 %gather_fusion.3 = f32[16,128,1024]{1,2,0:T(8,128)} fusion(f32[8,128,1024]{1,2,0:T(8,128)} %get-tuple-element.9, s32[1024]{0:T(1024)S(1)} %pad_clamp_fusion), kind=kCustom, calls=%fused_computation.3 | custom fusion | bytes 16777280 | tf_op jit(solution)/shard_map/gather | solution.py:50
  250.1 8.9 %copy.28 = f32[2,8,128,8,128]{4,3,2,1,0:T(8,128)} copy(f32[2,8,128,8,128]{2,4,3,1,0:T(8,128)} %bitcast.59) | data formatting | bytes 16777216 | tf_op jit(solution)/shard_map/reshape | solution.py:50
  259.0 10.5 %convolution_bitcast_fusion.1 = f32[2,8,128,8,128]{4,3,2,1,0:T(8,128)} fusion(f32[2,8,128,8,128]{4,3,2,1,0:T(8,128)} %copy.28, s32[2,8]{1,0:T(2,128)S(1)} %copy.24, s32[2,8,8]{2,1,0:T(8,128)S(1)} %bitcast.69), kind=kOutput, calls=%fused_computation.11 | convolution fusion | flops 201327616 | bytes 16777792 | tf_op jit(solution)/shard_map/skimj,skpm->skipj/dot_general | solution.py:51
  269.5 9.3 %reshape.228 = f32[2,1024,1024]{2,1,0:T(8,128)} reshape(f32[2,8,128,8,128]{4,3,2,1,0:T(8,128)} %convolution_bitcast_fusion.1) | data formatting | bytes 16777216 | tf_op jit(solution)/shard_map/reshape | solution.py:52
  278.9 15.6 %fusion = f32[2,128,1024]{1,2,0:T(8,128)S(1)} fusion(f32[2,1024,1024]{2,1,0:T(8,128)} %reshape.228, f32[2,128,1024]{2,1,0:T(8,128)S(1)} %copy-done.1, f32[2,1024]{1,0:T(2,128)S(1)} %bitcast.72), kind=kOutput, calls=%fused_computation.16 | convolution fusion | flops 3221487616 | bytes 10493952 | tf_op jit(solution)/shard_map/sik,skn->sin/dot_general | solution.py:53
  294.5 1.3 copy.32
  (11 shorter events, 0.1 us)
Async XLA Ops:
  0.6 29.0 %collective-permute-start.2 = (f32[2,128,1024]{2,1,0:T(8,128)}, f32[2,128,1024]{2,1,0:T(8,128)S(1)}, u32[]{:S(2)}, u32[]{:S(2)}) collective-permute-start(f32[2,128,1024]{2,1,0:T(8,128)} %param.5), channel_id=1, source_target_pairs={{1,0},{2,1},{3,2},{4,3},{5,4},{6,5},{7,6},{0,7},{9,8},{10,9},{11,1... | collective-permute-start | bytes 3145736 | tf_op jit(solution)/shard_map/ppermute | solution.py:26
  5.7 45.2 %collective-permute-start.1 = (f32[2,128,1024]{2,1,0:T(8,128)}, f32[2,128,1024]{2,1,0:T(8,128)}, u32[]{:S(2)}, u32[]{:S(2)}) collective-permute-start(f32[2,128,1024]{2,1,0:T(8,128)} %param.5), channel_id=1, source_target_pairs={{8,0},{16,8},{24,16},{32,24},{40,32},{48,40},{56,48},{64,56},{72,6... | collective-permute-start | bytes 3145736 | tf_op jit(solution)/shard_map/ppermute | solution.py:18
  10.1 45.3 %collective-permute-start = (f32[2,128,1024]{2,1,0:T(8,128)}, f32[2,128,1024]{2,1,0:T(8,128)}, u32[]{:S(2)}, u32[]{:S(2)}) collective-permute-start(f32[2,128,1024]{2,1,0:T(8,128)} %param.5), channel_id=1, source_target_pairs={{0,8},{8,16},{16,24},{24,32},{32,40},{40,48},{48,56},{56,64},{64,7... | collective-permute-start | bytes 3145736 | tf_op jit(solution)/shard_map/ppermute | solution.py:15
  78.3 9.3 %copy-start = (f32[2,128,1024]{2,1,0:T(8,128)S(1)}, f32[2,128,1024]{2,1,0:T(8,128)}, u32[]{:S(2)}) copy-start(f32[2,128,1024]{2,1,0:T(8,128)} %param.6) | copy-start | bytes 3145732
  103.4 46.4 %collective-permute-start.5 = (f32[2,2,128,1024]{2,3,1,0:T(8,128)S(1)}, f32[2,2,128,1024]{2,3,1,0:T(8,128)S(1)}, u32[]{:S(2)}, u32[]{:S(2)}) collective-permute-start(f32[2,2,128,1024]{2,3,1,0:T(8,128)S(1)} %pad_maximum_fusion.2), channel_id=1, source_target_pairs={{1,0},{2,1},{3,2},{4,3},{5,4},{6,5},{7,6},{0,7},{9,8},{10,9},{11,1... | collective-permute-start | bytes 6291464 | tf_op jit(solution)/shard_map/ppermute | solution.py:26
  103.5 89.1 %collective-permute-start.4 = (f32[2,2,128,1024]{2,3,1,0:T(8,128)S(1)}, f32[2,2,128,1024]{2,3,1,0:T(8,128)S(1)}, u32[]{:S(2)}, u32[]{:S(2)}) collective-permute-start(f32[2,2,128,1024]{2,3,1,0:T(8,128)S(1)} %pad_maximum_fusion.2), channel_id=1, source_target_pairs={{8,0},{16,8},{24,16},{32,24},{40,32},{48,40},{56,48},{64,56},{72,6... | collective-permute-start | bytes 6291464 | tf_op jit(solution)/shard_map/ppermute | solution.py:18
  104.6 91.0 %collective-permute-start.3 = (f32[2,2,128,1024]{2,3,1,0:T(8,128)S(1)}, f32[2,2,128,1024]{2,3,1,0:T(8,128)S(1)}, u32[]{:S(2)}, u32[]{:S(2)}) collective-permute-start(f32[2,2,128,1024]{2,3,1,0:T(8,128)S(1)} %pad_maximum_fusion.2), channel_id=1, source_target_pairs={{0,8},{8,16},{16,24},{24,32},{32,40},{40,48},{48,56},{56,64},{64,7... | collective-permute-start | bytes 6291464 | tf_op jit(solution)/shard_map/ppermute | solution.py:15
  269.5 9.3 %copy-start.1 = (f32[2,128,1024]{2,1,0:T(8,128)S(1)}, f32[2,128,1024]{2,1,0:T(8,128)}, u32[]{:S(2)}) copy-start(f32[2,128,1024]{2,1,0:T(8,128)} %param.5) | copy-start | bytes 3145732
where the time goes:
time: 302 us; the launch traced here: 296 us
  waiting for transfers between devices  128 us (42%)
  local copies, waits for them, and re-layouts  81.2 us (27%)
  matrix products  66.9 us (22%)
  starting transfers between devices  10.6 us (4%)
  other arithmetic  8 us (3%)
    ppermute x2, waiting for transfers between devices, with_halo(): lax.ppermute(lax.slice_in_dim(block, 0, width, axis=dim), axis, backward)  64.1 us
    ppermute x2, waiting for transfers between devices, shifted(): return lax.ppermute(block, axis, route)  56.7 us
    dot_general x3, matrix products, filtered_product(): jnp.einsum('sik,skn->sin', left_factor, chosen, precision=PRECISE, prefer...  39.3 us
    reshape x3, local copies, waits for them, and re-layouts, filtered_product(): chosen = chosen.reshape(rows_dev, row_width, row_width)  27.9 us
    dot_general x3, matrix products, filtered_product(): jnp.einsum('skimj,skpm->skipj', picked, selector, precision=PRECISE)  27.6 us
    gather x3, local copies, waits for them, and re-layouts, filtered_product(): extended[ext_index]  19.5 us
    reshape x2, local copies, waits for them, and re-layouts, filtered_product(): extended[ext_index]  17.5 us
    unnamed x10, local copies, waits for them, and re-layouts  9.22 us
  transfers between devices with their start and end apart: 6, of which 6 were waited for; matrix products, arithmetic and copies ran while one was open for 3% of the time, Pallas kernels for 0%

commit v1 on v0

v1 whole, which is shorter than its diff:
```python
import functools

import jax
import jax.numpy as jnp
from jax import lax
from jax.experimental import pallas as pl
from jax.experimental.pallas import tpu as pltpu
from jax.sharding import PartitionSpec as P

MESH = pl.DeviceIdType.MESH
BLK = 128
ROWS = 2
SLOTS = 8
UNIT = ROWS * BLK

OWN, NEAR, FAR, SIDE = 0, 1, 2, 3

(Y_NO, Y_NN, Z_NO, Z_NN, T_NO, T_NN,
 Y_XO, Y_XX, Z_XO, Z_XX, T_XX,
 Y_SS, Z_SS, T_SS) = range(14)


def split(value):
    high = value.astype(jnp.bfloat16)
    low = (value - high.astype(jnp.float32)).astype(jnp.bfloat16)
    return high, low


def kernel(row_count, col_count, pat_ref, keep_ref, y_ref, z_ref, yn_ref, zn_ref,
           own_y, own_z, own_t, recv, yh, yl, zh, zl, th, tl, rh, rl, acc_y, acc_z,
           send_sem, recv_sem):
    row = lax.axis_index("row")
    col = lax.axis_index("col")
    odd = lax.rem(row, 2)
    near = (row + 1 - 2 * odd, col)
    far = (lax.rem(row + row_count - 1 + 2 * odd, row_count), col)
    side = (row, lax.rem(col + 1, col_count))
    back = (row, lax.rem(col + col_count - 1, col_count))

    barrier = pltpu.get_barrier_semaphore()
    for other in (near, far, side, back):
        pl.semaphore_signal(barrier, inc=1, device_id=other, device_id_type=MESH)

    def first(place):
        return (place[0] * col_count + place[1]) * ROWS

    starts = [first(place) for place in ((row, col), near, far, side)]
    labels = [pat_ref[0, starts[q // ROWS] + q % ROWS] for q in range(SLOTS)]

    def pick(wanted, keys, values):
        found = values[0]
        for key, value in zip(keys[1:], values[1:]):
            found = jnp.where(key == wanted, value, found)
        return found

    numbers = [jnp.int32(k) for k in range(SLOTS)]
    keys = [[pat_ref[k, starts[OWN] + s] for k in range(SLOTS)] for s in range(ROWS)]
    keep = [[jnp.float32(1)] + [keep_ref[k, starts[OWN] + s].astype(jnp.float32) for k in range(1, SLOTS)]
            for s in range(ROWS)]
    slot_of = [[pick(labels[q], keys[s], numbers) for q in range(SLOTS)] for s in range(ROWS)]
    place_of = [[pick(keys[s][k], labels, numbers) for k in range(SLOTS)] for s in range(ROWS)]
    kept = [[pick(labels[q], keys[s], keep[s]) for q in range(SLOTS)] for s in range(ROWS)]
    kept_far = []
    for s in range(ROWS):
        far_keys = [pat_ref[k, starts[FAR] + s] for k in range(SLOTS)]
        far_keep = [keep_ref[k, starts[FAR] + s].astype(jnp.float32) for k in range(SLOTS)]
        kept_far.append([pick(labels[e], far_keys, far_keep) for e in range(ROWS)])

    def same(value, number):
        return jnp.full((BLK, BLK), value, jnp.int32) == number

    def blk(s, e):
        return pl.ds(s * BLK, BLK), pl.ds(e * BLK, BLK)

    for source, whole, high, low in ((y_ref, own_y, yh, yl), (z_ref, own_z, zh, zl)):
        for g in range(4):
            for s in range(ROWS):
                for e in range(ROWS):
                    slot = slot_of[s][g * ROWS + e]
                    value = source[s, :, pl.ds(0, BLK)]
                    for k in range(1, SLOTS):
                        value = jnp.where(same(slot, k), source[s, :, pl.ds(k * BLK, BLK)], value)
                    h, l = split(value)
                    where = (g, *blk(s, e))
                    whole[where] = value
                    high[where] = h
                    low[where] = l

    pl.semaphore_wait(barrier, 4)

    copies = {}

    def send(source, unit, target):
        copy = pltpu.make_async_remote_copy(
            src_ref=source, dst_ref=recv.at[unit], send_sem=send_sem.at[unit],
            recv_sem=recv_sem.at[unit], device_id=target, device_id_type=MESH)
        copy.start()
        copies[unit] = copy

    send(own_y.at[FAR], Y_XO, far)
    send(own_y.at[OWN], Y_SS, back)
    send(own_y.at[NEAR], Y_NO, near)
    send(own_y.at[OWN], Y_XX, far)
    send(own_z.at[OWN], Z_SS, back)
    send(own_y.at[OWN], Y_NN, near)
    send(own_z.at[FAR], Z_XO, far)
    send(own_z.at[NEAR], Z_NO, near)
    send(own_z.at[OWN], Z_XX, far)
    send(own_z.at[OWN], Z_NN, near)

    def arrive(unit):
        copies[unit].wait_recv()
        h, l = split(recv[unit])
        rh[unit] = h
        rl[unit] = l

    def mul(a_high, a_low, b_high, b_low):
        dot = functools.partial(jnp.dot, preferred_element_type=jnp.float32)
        return dot(a_high, b_high) + (dot(a_high, b_low) + dot(a_low, b_high))

    Y = lambda g: (yh[g], yl[g])
    Z = lambda g: (zh[g], zl[g])
    T = lambda g: (th[g], tl[g])
    R = lambda u: (rh[u], rl[u])

    def factor_of(product, region, s, e):
        value = (-0.5 * kept[s][region * ROWS + e]) * product[s * BLK:(s + 1) * BLK, e * BLK:(e + 1) * BLK]
        if region == OWN and s == e:
            eye = lax.broadcasted_iota(jnp.int32, (BLK, BLK), 0) == lax.broadcasted_iota(jnp.int32, (BLK, BLK), 1)
            value = value + jnp.where(eye, jnp.float32(1.5), jnp.float32(0))
        return value

    def set_factor(region, product):
        for s in range(ROWS):
            for e in range(ROWS):
                value = factor_of(product, region, s, e)
                h, l = split(value)
                where = (region, *blk(s, e))
                th[where] = h
                tl[where] = l
                if region in (OWN, NEAR):
                    own_t[where] = value

    def parts(g):
        return [(g * ROWS + e, s, blk_of(s, e)) for s in range(ROWS) for e in range(ROWS)]

    def blk_of(s, e):
        return slice(s * BLK, (s + 1) * BLK), slice(e * BLK, (e + 1) * BLK)

    def put(acc, g, value):
        for q, s, where in parts(g):
            acc[q, s] = value[where]

    def add(acc, g, value):
        for q, s, where in parts(g):
            acc[q, s] += value[where]

    def get(acc, g):
        rows = [jnp.concatenate([acc[g * ROWS + e, s] for e in range(ROWS)], axis=1) for s in range(ROWS)]
        return jnp.concatenate(rows, axis=0)

    arrive(Y_NO)
    put(acc_z, OWN, mul(*Z(OWN), *Y(OWN)) + mul(*Z(NEAR), *R(Y_NO)))
    arrive(Y_NN)
    set_factor(NEAR, mul(*Z(OWN), *Y(NEAR)) + mul(*Z(NEAR), *R(Y_NN)))
    send(own_t.at[NEAR], T_NO, near)
    put(acc_z, FAR, mul(*Z(OWN), *Y(FAR)))
    put(acc_z, SIDE, mul(*Z(OWN), *Y(SIDE)))
    put(acc_y, NEAR, mul(*Y(OWN), *T(NEAR)))
    arrive(Y_XO)
    set_factor(OWN, get(acc_z, OWN) + mul(*Z(FAR), *R(Y_XO)))
    arrive(Z_NO)
    arrive(Z_NN)
    send(own_t.at[OWN], T_XX, far)
    send(own_t.at[OWN], T_SS, back)
    send(own_t.at[OWN], T_NN, near)
    put(acc_y, OWN, mul(*Y(OWN), *T(OWN)))
    put(acc_z, OWN, mul(*T(OWN), *Z(OWN)) + mul(*T(NEAR), *R(Z_NO)))
    put(acc_z, NEAR, mul(*T(OWN), *Z(NEAR)) + mul(*T(NEAR), *R(Z_NN)))
    arrive(T_NO)
    add(acc_y, OWN, mul(*Y(NEAR), *R(T_NO)))
    arrive(Y_SS)
    set_factor(SIDE, get(acc_z, SIDE) + mul(*Z(SIDE), *R(Y_SS)))
    put(acc_z, SIDE, mul(*T(OWN), *Z(SIDE)))
    put(acc_y, SIDE, mul(*Y(OWN), *T(SIDE)))
    arrive(T_NN)
    add(acc_y, NEAR, mul(*Y(NEAR), *R(T_NN)))
    arrive(Y_XX)
    set_factor(FAR, get(acc_z, FAR) + mul(*Z(FAR), *R(Y_XX)))
    put(acc_z, FAR, mul(*T(OWN), *Z(FAR)))
    put(acc_y, FAR, mul(*Y(OWN), *T(FAR)))
    arrive(Z_SS)
    add(acc_z, SIDE, mul(*T(SIDE), *R(Z_SS)))
    arrive(Z_XO)
    add(acc_z, OWN, mul(*T(FAR), *R(Z_XO)))
    arrive(Z_XX)
    add(acc_z, FAR, mul(*T(FAR), *R(Z_XX)))
    other = mul(*R(Z_XX), *R(Y_XO)) + mul(*R(Z_XO), *Y(OWN))
    for s in range(ROWS):
        for e in range(ROWS):
            value = (-0.5 * kept_far[s][e]) * other[s * BLK:(s + 1) * BLK, e * BLK:(e + 1) * BLK]
            h, l = split(value)
            rh[(Z_XX, *blk(s, e))] = h
            rl[(Z_XX, *blk(s, e))] = l
    add(acc_y, OWN, mul(*Y(FAR), *R(Z_XX)))

    def emit(result, out):
        for s in range(ROWS):
            for p in range(SLOTS):
                out[s, :, pl.ds(p * BLK, BLK)] = keep[s][p] * result[place_of[s][p], s]

    emit(acc_z, zn_ref)
    arrive(T_SS)
    add(acc_y, SIDE, mul(*Y(SIDE), *R(T_SS)))
    arrive(T_XX)
    add(acc_y, FAR, mul(*Y(FAR), *R(T_XX)))
    emit(acc_y, yn_ref)
    for copy in copies.values():
        copy.wait_send()


def local(row_count, col_count, sqrt_iterate, inverse_iterate, pattern, keep_mask, row_order):
    del row_order
    whole = jax.ShapeDtypeStruct(sqrt_iterate.shape, jnp.float32)
    unit = (UNIT, UNIT)
    vmem = pl.BlockSpec(memory_space=pltpu.VMEM)
    smem = pl.BlockSpec(memory_space=pltpu.SMEM)
    f32 = lambda n: pltpu.VMEM((n, *unit), jnp.float32)
    b16 = lambda n: pltpu.VMEM((n, *unit), jnp.bfloat16)
    return pl.pallas_call(
        functools.partial(kernel, row_count, col_count),
        out_shape=(whole, whole),
        in_specs=[smem, smem, vmem, vmem],
        out_specs=(vmem, vmem),
        scratch_shapes=[
            f32(4), f32(4), f32(2), f32(14),
            b16(4), b16(4), b16(4), b16(4), b16(4), b16(4), b16(14), b16(14),
            pltpu.VMEM((SLOTS, ROWS, BLK, BLK), jnp.float32),
            pltpu.VMEM((SLOTS, ROWS, BLK, BLK), jnp.float32),
            pltpu.SemaphoreType.DMA((14,)),
            pltpu.SemaphoreType.DMA((14,)),
        ],
        compiler_params=pltpu.CompilerParams(
            collective_id=0, has_side_effects=True, vmem_limit_bytes=48 << 20),
    )(pattern.T, keep_mask.T, sqrt_iterate, inverse_iterate)


def solution(mesh):
    split_rows = P(("row", "col"), None, None)
    body = functools.partial(local, mesh.shape["row"], mesh.shape["col"])
    return jax.shard_map(
        body, mesh=mesh, in_specs=(split_rows, split_rows, P(), P(), P()),
        out_specs=(split_rows, split_rows), check_vma=False)
```

time: 302 us -> 58.1 us (0.19); the launches traced: 296 us -> 57.4 us
  waiting for transfers between devices: 128 us -> 0 us
  local copies, waits for them, and re-layouts: 81.2 us -> 5.78 us
  matrix products: 66.9 us -> 0 us
  Pallas kernels: 0 us -> 51 us
  starting transfers between devices: 10.6 us -> 0 us
  other arithmetic: 8 us -> 0 us
    ppermute x6 -> x0, waiting for transfers between devices: 128 us -> none  [the longest x2 64.1 us: with_halo(): lax.ppermute(lax.slice_in_dim(block, 0, width, axis=dim), axis, backward)]
    dot_general x6 -> x0, matrix products: 66.9 us -> none  [the longest x3 39.3 us: filtered_product(): jnp.einsum('sik,skn->sin', left_factor, chosen, precision=PRECISE, prefer...]
    pallas_call x0 -> x1, Pallas kernels: none -> 51 us  [local(): pl.pallas_call(functools.partial(kernel, row_count, col_count), out_shape...]
    reshape x5 -> x0, local copies, waits for them, and re-layouts: 45.4 us -> none  [the longest x3 27.9 us: filtered_product(): chosen = chosen.reshape(rows_dev, row_width, row_width)]
    gather x6 -> x0, local copies, waits for them, and re-layouts: 20.8 us -> none  [the longest x3 19.5 us: filtered_product(): extended[ext_index]]
    ppermute x6 -> x0, starting transfers between devices: 10.6 us -> none  [the longest x2 5.45 us: with_halo(): lax.ppermute(lax.slice_in_dim(block, 0, width, axis=dim), axis, backward)]
    concatenate x2 -> x0, other arithmetic: 5.52 us -> none  [the longest x1 4.34 us: local(): around_sqrt = jnp.concatenate([cycle_sqrt, side_sqrt], axis=0)]
    squeeze x1 -> x0, local copies, waits for them, and re-layouts: 3.82 us -> none  [local(): around_inverse = around_pair[1]]
  transfers between devices with their start and end apart: 6 -> 0, of which waited for: 6 -> 0; matrix products, arithmetic and copies ran while one was open for 3% -> 0% of each run, Pallas kernels for 0% -> 0%
where the time goes in v1:
time: 58.1 us; the launch traced here: 57.4 us
  Pallas kernels  51 us (88%)
  local copies, waits for them, and re-layouts  5.78 us (10%)
  between operations  0.65 us (1%)
    pallas_call x1, Pallas kernels, local(): pl.pallas_call(functools.partial(kernel, row_count, col_count), out_shape...  51 us
    unnamed x10, local copies, waits for them, and re-layouts  5.78 us

profile of v1, /device:TPU:0, one launch (start us, length us, event | category | flops | bytes accessed | tf_op | source)
XLA Modules:
  0.0 57.4 jit_solution(14806337215406245094)
XLA Ops:
  0.6 0.0 copy-start
  0.6 1.2 %copy-done = f32[2,128,1024]{2,1,0:T(8,128)S(1)} copy-done((f32[2,128,1024]{2,1,0:T(8,128)S(1)}, f32[2,128,1024]{2,1,0:T(8,128)}, u32[]{:S(2)}) %copy-start) | copy-done | bytes 1048600
  1.9 0.0 copy-start.1
  1.9 1.2 %copy-done.1 = f32[2,128,1024]{2,1,0:T(8,128)S(1)} copy-done((f32[2,128,1024]{2,1,0:T(8,128)S(1)}, f32[2,128,1024]{2,1,0:T(8,128)}, u32[]{:S(2)}) %copy-start.1) | copy-done | bytes 1048600
  3.1 0.0 copy-start.2
  3.1 0.7 %copy-done.2 = s32[256,8]{0,1:T(8,128)S(1)} copy-done((s32[256,8]{0,1:T(8,128)S(1)}, s32[256,8]{0,1:T(8,128)}, u32[]{:S(2)}) %copy-start.2) | copy-done | bytes 8216
  3.8 0.0 copy-start.3
  3.8 0.7 %copy-done.3 = s32[256,8]{0,1:T(8,128)S(1)} copy-done((s32[256,8]{0,1:T(8,128)S(1)}, s32[256,8]{0,1:T(8,128)}, u32[]{:S(2)}) %copy-start.3) | copy-done | bytes 8216
  4.5 51.0 %shard_map.59 = (f32[2,128,1024]{2,1,0:T(8,128)S(1)}, f32[2,128,1024]{2,1,0:T(8,128)S(1)}) custom-call(s32[8,256]{1,0:T(8,128)S(1)} %bitcast.2, s32[8,256]{1,0:T(8,128)S(1)} %bitcast.3, f32[2,128,1024]{2,1,0:T(8,128)S(1)} %copy-done, f32[2,128,1024]{2,1,0:T(8,128)S(1)} %copy-done.1), custom_call_target="tpu_custom_call" | custom-call | tf_op jit(solution)/shard_map/pallas_call | solution.py:230
  55.5 1.0 %copy.8 = f32[2,128,1024]{2,1,0:T(8,128)} copy(f32[2,128,1024]{2,1,0:T(8,128)S(1)} %get-tuple-element.4) | data formatting | bytes 2097152
  56.5 1.0 %copy.9 = f32[2,128,1024]{2,1,0:T(8,128)} copy(f32[2,128,1024]{2,1,0:T(8,128)S(1)} %get-tuple-element.5) | data formatting | bytes 2097152
Async XLA Ops:
  0.6 1.2 %copy-start = (f32[2,128,1024]{2,1,0:T(8,128)S(1)}, f32[2,128,1024]{2,1,0:T(8,128)}, u32[]{:S(2)}) copy-start(f32[2,128,1024]{2,1,0:T(8,128)} %y_ref.1) | copy-start | bytes 3145732
  1.9 1.2 %copy-start.1 = (f32[2,128,1024]{2,1,0:T(8,128)S(1)}, f32[2,128,1024]{2,1,0:T(8,128)}, u32[]{:S(2)}) copy-start(f32[2,128,1024]{2,1,0:T(8,128)} %z_ref.1) | copy-start | bytes 3145732
  3.1 0.7 %copy-start.2 = (s32[256,8]{0,1:T(8,128)S(1)}, s32[256,8]{0,1:T(8,128)}, u32[]{:S(2)}) copy-start(s32[256,8]{0,1:T(8,128)} %param.7) | copy-start | bytes 24580
  3.8 0.7 %copy-start.3 = (s32[256,8]{0,1:T(8,128)S(1)}, s32[256,8]{0,1:T(8,128)}, u32[]{:S(2)}) copy-start(s32[256,8]{0,1:T(8,128)} %param.8) | copy-start | bytes 24580

commit v2 on v1

--- a/solution.py
+++ b/solution.py
@@ -15,9 +15,13 @@
 
 OWN, NEAR, FAR, SIDE = 0, 1, 2, 3
 
+RUN = 4
+CHUNK = UNIT // RUN
+
 (Y_NO, Y_NN, Z_NO, Z_NN, T_NO, T_NN,
  Y_XO, Y_XX, Z_XO, Z_XX, T_XX,
  Y_SS, Z_SS, T_SS) = range(14)
+SIDES = (Y_SS, Z_SS, T_SS)
 
 
 def split(value):
@@ -26,9 +30,17 @@
     return high, low
 
 
-def kernel(row_count, col_count, pat_ref, keep_ref, y_ref, z_ref, yn_ref, zn_ref,
-           own_y, own_z, own_t, recv, yh, yl, zh, zl, th, tl, rh, rl, acc_y, acc_z,
-           send_sem, recv_sem):
+def kernel(row_count, col_count, pat_hbm, keep_hbm, y_hbm, z_hbm, yn_ref, zn_ref,
+           pat_ref, keep_ref, y_ref, z_ref,
+           own_y, own_z, own_t, recv, relay, yh, yl, zh, zl, th, tl, rh, rl, acc_y, acc_z,
+           send_sem, recv_sem, side_send, side_recv, relay_send, relay_recv, load_sem):
+    loads = [
+        pltpu.make_async_copy(source, target, load_sem.at[i])
+        for i, (source, target) in enumerate((
+            (pat_hbm, pat_ref), (keep_hbm, keep_ref), (y_hbm, y_ref), (z_hbm, z_ref)))
+    ]
+    for load in loads:
+        load.start()
     row = lax.axis_index("row")
     col = lax.axis_index("col")
     odd = lax.rem(row, 2)
@@ -36,10 +48,15 @@
     far = (lax.rem(row + row_count - 1 + 2 * odd, row_count), col)
     side = (row, lax.rem(col + 1, col_count))
     back = (row, lax.rem(col + col_count - 1, col_count))
+    place = lax.rem(col, RUN)
+    wrap = (row, lax.rem(col - place + col_count - 1, col_count))
 
     barrier = pltpu.get_barrier_semaphore()
-    for other in (near, far, side, back):
+    peers = [(row, lax.rem(col + d, col_count)) for d in range(1, col_count)]
+    for other in [near, far] + peers:
         pl.semaphore_signal(barrier, inc=1, device_id=other, device_id_type=MESH)
+    loads[0].wait()
+    loads[1].wait()
 
     def first(place):
         return (place[0] * col_count + place[1]) * ROWS
@@ -72,7 +89,9 @@
     def blk(s, e):
         return pl.ds(s * BLK, BLK), pl.ds(e * BLK, BLK)
 
-    for source, whole, high, low in ((y_ref, own_y, yh, yl), (z_ref, own_z, zh, zl)):
+    for load, source, whole, high, low in (
+            (loads[2], y_ref, own_y, yh, yl), (loads[3], z_ref, own_z, zh, zl)):
+        load.wait()
         for g in range(4):
             for s in range(ROWS):
                 for e in range(ROWS):
@@ -86,7 +105,7 @@
                     high[where] = h
                     low[where] = l
 
-    pl.semaphore_wait(barrier, 4)
+    pl.semaphore_wait(barrier, 1 + col_count)
 
     copies = {}
 
@@ -97,19 +116,67 @@
         copy.start()
         copies[unit] = copy
 
+    def chunk(j):
+        return pl.ds(j * CHUNK, CHUNK)
+
+    def side_copy(source, number, j):
+        return pltpu.make_async_remote_copy(
+            src_ref=source.at[chunk(j)], dst_ref=recv.at[SIDES[number], chunk(j)],
+            send_sem=side_send.at[number, j], recv_sem=side_recv.at[number, j],
+            device_id=back, device_id_type=MESH)
+
+    def detour_copy(source, number, j):
+        return pltpu.make_async_remote_copy(
+            src_ref=source.at[chunk(j)], dst_ref=relay.at[number],
+            send_sem=side_send.at[number, j], recv_sem=relay_recv.at[number],
+            device_id=(row, col + j), device_id_type=MESH)
+
+    def relay_copy(number):
+        return pltpu.make_async_remote_copy(
+            src_ref=relay.at[number], dst_ref=recv.at[SIDES[number], chunk(place)],
+            send_sem=relay_send.at[number], recv_sem=side_recv.at[number, place],
+            device_id=wrap, device_id_type=MESH)
+
+    def send_side(source, number):
+        @pl.when(place == 0)
+        def _():
+            for j in range(1, RUN):
+                detour_copy(source, number, j).start()
+
+        side_copy(source, number, 0).start()
+
+        @pl.when(place != 0)
+        def _():
+            for j in range(1, RUN):
+                side_copy(source, number, j).start()
+
+    def pass_on(number):
+        @pl.when(place != 0)
+        def _():
+            pltpu.make_async_remote_copy(
+                src_ref=own_y.at[OWN, chunk(0)], dst_ref=relay.at[number],
+                send_sem=side_send.at[number, 0], recv_sem=relay_recv.at[number],
+                device_id=back, device_id_type=MESH).wait_recv()
+            relay_copy(number).start()
+
     send(own_y.at[FAR], Y_XO, far)
-    send(own_y.at[OWN], Y_SS, back)
+    send(own_y.at[OWN], Y_XX, far)
+    send(own_z.at[FAR], Z_XO, far)
+    send(own_z.at[OWN], Z_XX, far)
     send(own_y.at[NEAR], Y_NO, near)
-    send(own_y.at[OWN], Y_XX, far)
-    send(own_z.at[OWN], Z_SS, back)
     send(own_y.at[OWN], Y_NN, near)
-    send(own_z.at[FAR], Z_XO, far)
+    send_side(own_y.at[OWN], 0)
+    send_side(own_z.at[OWN], 1)
     send(own_z.at[NEAR], Z_NO, near)
-    send(own_z.at[OWN], Z_XX, far)
     send(own_z.at[OWN], Z_NN, near)
 
     def arrive(unit):
-        copies[unit].wait_recv()
+        if unit in SIDES:
+            number = SIDES.index(unit)
+            for j in range(RUN):
+                side_copy(own_y.at[OWN], number, j).wait_recv()
+        else:
+            copies[unit].wait_recv()
         h, l = split(recv[unit])
         rh[unit] = h
         rl[unit] = l
@@ -167,32 +234,35 @@
     put(acc_z, FAR, mul(*Z(OWN), *Y(FAR)))
     put(acc_z, SIDE, mul(*Z(OWN), *Y(SIDE)))
     put(acc_y, NEAR, mul(*Y(OWN), *T(NEAR)))
+    pass_on(0)
+    pass_on(1)
     arrive(Y_XO)
     set_factor(OWN, get(acc_z, OWN) + mul(*Z(FAR), *R(Y_XO)))
     arrive(Z_NO)
     arrive(Z_NN)
     send(own_t.at[OWN], T_XX, far)
-    send(own_t.at[OWN], T_SS, back)
+    send_side(own_t.at[OWN], 2)
     send(own_t.at[OWN], T_NN, near)
     put(acc_y, OWN, mul(*Y(OWN), *T(OWN)))
     put(acc_z, OWN, mul(*T(OWN), *Z(OWN)) + mul(*T(NEAR), *R(Z_NO)))
     put(acc_z, NEAR, mul(*T(OWN), *Z(NEAR)) + mul(*T(NEAR), *R(Z_NN)))
     arrive(T_NO)
     add(acc_y, OWN, mul(*Y(NEAR), *R(T_NO)))
-    arrive(Y_SS)
-    set_factor(SIDE, get(acc_z, SIDE) + mul(*Z(SIDE), *R(Y_SS)))
-    put(acc_z, SIDE, mul(*T(OWN), *Z(SIDE)))
-    put(acc_y, SIDE, mul(*Y(OWN), *T(SIDE)))
+    pass_on(2)
     arrive(T_NN)
     add(acc_y, NEAR, mul(*Y(NEAR), *R(T_NN)))
     arrive(Y_XX)
     set_factor(FAR, get(acc_z, FAR) + mul(*Z(FAR), *R(Y_XX)))
     put(acc_z, FAR, mul(*T(OWN), *Z(FAR)))
     put(acc_y, FAR, mul(*Y(OWN), *T(FAR)))
+    arrive(Z_XO)
+    add(acc_z, OWN, mul(*T(FAR), *R(Z_XO)))
+    arrive(Y_SS)
+    set_factor(SIDE, get(acc_z, SIDE) + mul(*Z(SIDE), *R(Y_SS)))
+    put(acc_z, SIDE, mul(*T(OWN), *Z(SIDE)))
+    put(acc_y, SIDE, mul(*Y(OWN), *T(SIDE)))
     arrive(Z_SS)
     add(acc_z, SIDE, mul(*T(SIDE), *R(Z_SS)))
-    arrive(Z_XO)
-    add(acc_z, OWN, mul(*T(FAR), *R(Z_XO)))
     arrive(Z_XX)
     add(acc_z, FAR, mul(*T(FAR), *R(Z_XX)))
     other = mul(*R(Z_XX), *R(Y_XO)) + mul(*R(Z_XO), *Y(OWN))
@@ -217,6 +287,27 @@
     emit(acc_y, yn_ref)
     for copy in copies.values():
         copy.wait_send()
+    for number in range(len(SIDES)):
+        for j in range(RUN):
+            side_copy(own_y.at[OWN], number, j).wait_send()
+
+    @pl.when(place != 0)
+    def _():
+        for number in range(len(SIDES)):
+            relay_copy(number).wait_send()
+
+
+def write_out(y_ref, z_ref, y_hbm, z_hbm, sem):
+    copies = []
+    for source, target in ((y_ref, y_hbm), (z_ref, z_hbm)):
+        for s in range(ROWS):
+            for part in range(2):
+                where = (s, pl.ds(part * (BLK // 2), BLK // 2))
+                copies.append(pltpu.make_async_copy(source.at[where], target.at[where], sem.at[len(copies)]))
+    for copy in copies:
+        copy.start()
+    for copy in copies:
+        copy.wait()
 
 
 def local(row_count, col_count, sqrt_iterate, inverse_iterate, pattern, keep_mask, row_order):
@@ -224,25 +315,36 @@
     whole = jax.ShapeDtypeStruct(sqrt_iterate.shape, jnp.float32)
     unit = (UNIT, UNIT)
     vmem = pl.BlockSpec(memory_space=pltpu.VMEM)
-    smem = pl.BlockSpec(memory_space=pltpu.SMEM)
     f32 = lambda n: pltpu.VMEM((n, *unit), jnp.float32)
     b16 = lambda n: pltpu.VMEM((n, *unit), jnp.bfloat16)
-    return pl.pallas_call(
+    hbm = pl.BlockSpec(memory_space=pltpu.HBM)
+    dma = pltpu.SemaphoreType.DMA
+    results = pl.pallas_call(
         functools.partial(kernel, row_count, col_count),
         out_shape=(whole, whole),
-        in_specs=[smem, smem, vmem, vmem],
+        in_specs=[hbm] * 4,
         out_specs=(vmem, vmem),
         scratch_shapes=[
-            f32(4), f32(4), f32(2), f32(14),
+            pltpu.SMEM(pattern.shape[::-1], jnp.int32), pltpu.SMEM(pattern.shape[::-1], jnp.int32),
+            pltpu.VMEM(whole.shape, jnp.float32), pltpu.VMEM(whole.shape, jnp.float32),
+            f32(4), f32(4), f32(2), f32(14), pltpu.VMEM((len(SIDES), CHUNK, UNIT), jnp.float32),
             b16(4), b16(4), b16(4), b16(4), b16(4), b16(4), b16(14), b16(14),
             pltpu.VMEM((SLOTS, ROWS, BLK, BLK), jnp.float32),
             pltpu.VMEM((SLOTS, ROWS, BLK, BLK), jnp.float32),
-            pltpu.SemaphoreType.DMA((14,)),
-            pltpu.SemaphoreType.DMA((14,)),
+            dma((14,)), dma((14,)), dma((len(SIDES), RUN)), dma((len(SIDES), RUN)),
+            dma((len(SIDES),)), dma((len(SIDES),)), dma((4,)),
         ],
         compiler_params=pltpu.CompilerParams(
-            collective_id=0, has_side_effects=True, vmem_limit_bytes=48 << 20),
+            collective_id=0, has_side_effects=True, vmem_limit_bytes=54_000_000),
     )(pattern.T, keep_mask.T, sqrt_iterate, inverse_iterate)
+    return pl.pallas_call(
+        write_out,
+        out_shape=(whole, whole),
+        in_specs=[vmem, vmem],
+        out_specs=(hbm, hbm),
+        scratch_shapes=[dma((8,))],
+        compiler_params=pltpu.CompilerParams(vmem_limit_bytes=4194304),
+    )(*results)
 
 
 def solution(mesh):

time: 58.1 us -> 45.5 us (0.78)
  Pallas kernels: 51 us -> 42.8 us
  local copies, waits for them, and re-layouts: 5.78 us -> 1.39 us
    pallas_call x1, Pallas kernels: 51 us -> 41.5 us  [local(): pl.pallas_call(functools.partial(kernel, row_count, col_count), out_shape...]
    unnamed x10 -> x4, local copies, waits for them, and re-layouts: 5.78 us -> 1.39 us
    pallas_call x0 -> x1, Pallas kernels: none -> 1.38 us  [local(): pl.pallas_call(write_out, out_shape=(whole, whole), in_specs=[vmem, vmem]...]
where the time goes in v2:
time: 45.5 us; the launch traced here: 44.9 us
  Pallas kernels  42.8 us (94%)
  local copies, waits for them, and re-layouts  1.39 us (3%)
  between operations  0.65 us (1%)
    pallas_call x1, Pallas kernels, local(): pl.pallas_call(functools.partial(kernel, row_count, col_count), out_shape...  41.5 us
    unnamed x4, local copies, waits for them, and re-layouts  1.39 us
    pallas_call x1, Pallas kernels, local(): pl.pallas_call(write_out, out_shape=(whole, whole), in_specs=[vmem, vmem]...  1.38 us

profile of v2, /device:TPU:0, one launch (start us, length us, event | category | flops | bytes accessed | tf_op | source)
XLA Modules:
  0.0 44.9 jit_solution(12625434317612824163)
XLA Ops:
  0.6 0.0 copy-start
  0.6 0.7 %copy-done = s32[256,8]{0,1:T(8,128)S(1)} copy-done((s32[256,8]{0,1:T(8,128)S(1)}, s32[256,8]{0,1:T(8,128)}, u32[]{:S(2)}) %copy-start) | copy-done | bytes 8216
  1.3 0.0 copy-start.1
  1.3 0.7 %copy-done.1 = s32[256,8]{0,1:T(8,128)S(1)} copy-done((s32[256,8]{0,1:T(8,128)S(1)}, s32[256,8]{0,1:T(8,128)}, u32[]{:S(2)}) %copy-start.1) | copy-done | bytes 8216
  2.0 41.5 %shard_map.59 = (f32[2,128,1024]{2,1,0:T(8,128)S(1)}, f32[2,128,1024]{2,1,0:T(8,128)S(1)}) custom-call(s32[8,256]{1,0:T(8,128)S(1)} %bitcast.2, s32[8,256]{1,0:T(8,128)S(1)} %bitcast.3, f32[2,128,1024]{2,1,0:T(8,128)} %y_hbm.1, f32[2,128,1024]{2,1,0:T(8,128)} %z_hbm.1), custom_call_target="tpu_custom_call" | custom-call | tf_op jit(solution)/shard_map/pallas_call | solution.py:322
  43.5 1.4 %shard_map.60 = (f32[2,128,1024]{2,1,0:T(8,128)}, f32[2,128,1024]{2,1,0:T(8,128)}) custom-call(f32[2,128,1024]{2,1,0:T(8,128)S(1)} %get-tuple-element.4.y_ref, f32[2,128,1024]{2,1,0:T(8,128)S(1)} %get-tuple-element.5.z_ref), custom_call_target="tpu_custom_call" | custom-call | tf_op jit(solution)/shard_map/pallas_call | solution.py:340
Async XLA Ops:
  0.6 0.7 %copy-start = (s32[256,8]{0,1:T(8,128)S(1)}, s32[256,8]{0,1:T(8,128)}, u32[]{:S(2)}) copy-start(s32[256,8]{0,1:T(8,128)} %param.7) | copy-start | bytes 24580
  1.3 0.7 %copy-start.1 = (s32[256,8]{0,1:T(8,128)S(1)}, s32[256,8]{0,1:T(8,128)}, u32[]{:S(2)}) copy-start(s32[256,8]{0,1:T(8,128)} %param.8) | copy-start | bytes 24580

commit v3 on v2

--- a/solution.py
+++ b/solution.py
@@ -16,12 +16,15 @@
 OWN, NEAR, FAR, SIDE = 0, 1, 2, 3
 
 RUN = 4
-CHUNK = UNIT // RUN
+PARTS = 4
+CHUNK = UNIT // PARTS
+HALF = UNIT // 2
 
 (Y_NO, Y_NN, Z_NO, Z_NN, T_NO, T_NN,
  Y_XO, Y_XX, Z_XO, Z_XX, T_XX,
  Y_SS, Z_SS, T_SS) = range(14)
 SIDES = (Y_SS, Z_SS, T_SS)
+FARS = (Y_XX, Z_XX, T_XX)
 
 
 def split(value):
@@ -32,8 +35,9 @@
 
 def kernel(row_count, col_count, pat_hbm, keep_hbm, y_hbm, z_hbm, yn_ref, zn_ref,
            pat_ref, keep_ref, y_ref, z_ref,
-           own_y, own_z, own_t, recv, relay, yh, yl, zh, zl, th, tl, rh, rl, acc_y, acc_z,
-           send_sem, recv_sem, side_send, side_recv, relay_send, relay_recv, load_sem):
+           own_y, own_z, own_t, recv, relay, bypass, cross, yh, yl, zh, zl, th, tl, rh, rl, acc_y, acc_z, acc_p,
+           send_sem, recv_sem, far_send, far_recv, side_send, side_recv, relay_send, relay_recv,
+           last_send, last_recv, bypass_sem, load_sem):
     loads = [
         pltpu.make_async_copy(source, target, load_sem.at[i])
         for i, (source, target) in enumerate((
@@ -49,11 +53,18 @@
     side = (row, lax.rem(col + 1, col_count))
     back = (row, lax.rem(col + col_count - 1, col_count))
     place = lax.rem(col, RUN)
-    wrap = (row, lax.rem(col - place + col_count - 1, col_count))
+    head = place == 0
+    first_col = col - place
+    twin_col = lax.rem(col + RUN, col_count)
+    twin = (row, twin_col)
+    twin_far = (far[0], twin_col)
+    twin_back = (row, lax.rem(twin_col + col_count - 1, col_count))
 
     barrier = pltpu.get_barrier_semaphore()
-    peers = [(row, lax.rem(col + d, col_count)) for d in range(1, col_count)]
-    for other in [near, far] + peers:
+    others = [near, twin_far]
+    others += [(row, lax.rem(col + d, col_count)) for d in range(1, col_count)]
+    others += [(far[0], first_col + d) for d in range(RUN)]
+    for other in others:
         pl.semaphore_signal(barrier, inc=1, device_id=other, device_id_type=MESH)
     loads[0].wait()
     loads[1].wait()
@@ -105,7 +116,7 @@
                     high[where] = h
                     low[where] = l
 
-    pl.semaphore_wait(barrier, 1 + col_count)
+    pl.semaphore_wait(barrier, len(others))
 
     copies = {}
 
@@ -119,62 +130,92 @@
     def chunk(j):
         return pl.ds(j * CHUNK, CHUNK)
 
-    def side_copy(source, number, j):
+    def remote(source, target, send_to, recv_from, device):
         return pltpu.make_async_remote_copy(
-            src_ref=source.at[chunk(j)], dst_ref=recv.at[SIDES[number], chunk(j)],
-            send_sem=side_send.at[number, j], recv_sem=side_recv.at[number, j],
-            device_id=back, device_id_type=MESH)
-
-    def detour_copy(source, number, j):
-        return pltpu.make_async_remote_copy(
-            src_ref=source.at[chunk(j)], dst_ref=relay.at[number],
-            send_sem=side_send.at[number, j], recv_sem=relay_recv.at[number],
-            device_id=(row, col + j), device_id_type=MESH)
-
-    def relay_copy(number):
-        return pltpu.make_async_remote_copy(
-            src_ref=relay.at[number], dst_ref=recv.at[SIDES[number], chunk(place)],
-            send_sem=relay_send.at[number], recv_sem=side_recv.at[number, place],
-            device_id=wrap, device_id_type=MESH)
-
-    def send_side(source, number):
-        @pl.when(place == 0)
-        def _():
-            for j in range(1, RUN):
-                detour_copy(source, number, j).start()
-
-        side_copy(source, number, 0).start()
-
-        @pl.when(place != 0)
-        def _():
-            for j in range(1, RUN):
-                side_copy(source, number, j).start()
-
-    def pass_on(number):
-        @pl.when(place != 0)
-        def _():
-            pltpu.make_async_remote_copy(
-                src_ref=own_y.at[OWN, chunk(0)], dst_ref=relay.at[number],
-                send_sem=side_send.at[number, 0], recv_sem=relay_recv.at[number],
-                device_id=back, device_id_type=MESH).wait_recv()
-            relay_copy(number).start()
+            src_ref=source, dst_ref=target, send_sem=send_to, recv_sem=recv_from,
+            device_id=device, device_id_type=MESH)
+
+    def far_copy(source, n, j):
+        return remote(source.at[chunk(j)], recv.at[FARS[n], chunk(j)], far_send.at[n, j], far_recv.at[n, j], far)
+
+    def side_copy(source, n, j):
+        return remote(source.at[chunk(j)], recv.at[SIDES[n], chunk(j)], side_send.at[n, j], side_recv.at[n, j], back)
+
+    def twin_copy(source, n, j):
+        return remote(source.at[chunk(j)], relay.at[n, chunk(j)], far_send.at[n, j], relay_recv.at[n, j], twin)
+
+    def on_far(n, j):
+        return remote(relay.at[n, chunk(j)], recv.at[FARS[n], chunk(j)], relay_send.at[n, j], far_recv.at[n, j], twin_far)
+
+    def on_side(n, j):
+        return remote(relay.at[n, chunk(j)], recv.at[SIDES[n], chunk(j)], side_send.at[n, j], side_recv.at[n, j], twin_back)
+
+    def send_own(source, n):
+        @pl.when(head)
+        def _():
+            for j in range(PARTS):
+                twin_copy(source, n, j).start()
+
+        @pl.when(jnp.logical_not(head))
+        def _():
+            for j in range(PARTS):
+                far_copy(source, n, j).start()
+            for j in range(PARTS):
+                side_copy(source, n, j).start()
+
+    def pass_on(n, chunks=range(PARTS)):
+        @pl.when(head)
+        def _():
+            for j in chunks:
+                twin_copy(own_y.at[OWN], n, j).wait_recv()
+                on_far(n, j).start()
+                on_side(n, j).start()
+
+    def last_copy(j):
+        return remote(own_z.at[FAR, chunk(j)], recv.at[Z_XO, chunk(j)], last_send.at[j], last_recv.at[j], far)
+
+    def detour_copy(j):
+        return remote(own_z.at[FAR, chunk(j)], bypass, last_send.at[j], bypass_sem.at[0], (row, col + j))
+
+    def on_detour():
+        return remote(bypass, recv.at[Z_XO, chunk(place)], bypass_sem.at[1], last_recv.at[place], (far[0], first_col))
+
+    def send_last_direct():
+        last_copy(0).start()
+
+        @pl.when(jnp.logical_not(head))
+        def _():
+            for j in range(1, PARTS):
+                last_copy(j).start()
+
+    def send_last_detour():
+        @pl.when(head)
+        def _():
+            for j in range(1, PARTS):
+                detour_copy(j).start()
+
+    def pass_detour():
+        @pl.when(jnp.logical_not(head))
+        def _():
+            detour_copy(0).wait_recv()
+            on_detour().start()
 
     send(own_y.at[FAR], Y_XO, far)
-    send(own_y.at[OWN], Y_XX, far)
-    send(own_z.at[FAR], Z_XO, far)
-    send(own_z.at[OWN], Z_XX, far)
+    send_last_detour()
+    send_own(own_y.at[OWN], 0)
+    send_own(own_z.at[OWN], 1)
     send(own_y.at[NEAR], Y_NO, near)
     send(own_y.at[OWN], Y_NN, near)
-    send_side(own_y.at[OWN], 0)
-    send_side(own_z.at[OWN], 1)
     send(own_z.at[NEAR], Z_NO, near)
     send(own_z.at[OWN], Z_NN, near)
 
     def arrive(unit):
         if unit in SIDES:
-            number = SIDES.index(unit)
-            for j in range(RUN):
-                side_copy(own_y.at[OWN], number, j).wait_recv()
+            for j in range(PARTS):
+                side_copy(own_y.at[OWN], SIDES.index(unit), j).wait_recv()
+        elif unit in FARS:
+            for j in range(PARTS):
+                far_copy(own_y.at[OWN], FARS.index(unit), j).wait_recv()
         else:
             copies[unit].wait_recv()
         h, l = split(recv[unit])
@@ -231,48 +272,59 @@
     arrive(Y_NN)
     set_factor(NEAR, mul(*Z(OWN), *Y(NEAR)) + mul(*Z(NEAR), *R(Y_NN)))
     send(own_t.at[NEAR], T_NO, near)
-    put(acc_z, FAR, mul(*Z(OWN), *Y(FAR)))
-    put(acc_z, SIDE, mul(*Z(OWN), *Y(SIDE)))
+    put(acc_p, FAR, mul(*Z(OWN), *Y(FAR)))
+    put(acc_p, SIDE, mul(*Z(OWN), *Y(SIDE)))
     put(acc_y, NEAR, mul(*Y(OWN), *T(NEAR)))
+    pass_detour()
     pass_on(0)
-    pass_on(1)
     arrive(Y_XO)
     set_factor(OWN, get(acc_z, OWN) + mul(*Z(FAR), *R(Y_XO)))
+    send_own(own_t.at[OWN], 2)
+    send(own_t.at[OWN], T_NN, near)
+    send_last_direct()
+    pass_on(1, range(0, 1))
     arrive(Z_NO)
     arrive(Z_NN)
-    send(own_t.at[OWN], T_XX, far)
-    send_side(own_t.at[OWN], 2)
-    send(own_t.at[OWN], T_NN, near)
     put(acc_y, OWN, mul(*Y(OWN), *T(OWN)))
     put(acc_z, OWN, mul(*T(OWN), *Z(OWN)) + mul(*T(NEAR), *R(Z_NO)))
+    pass_on(1, range(1, 2))
     put(acc_z, NEAR, mul(*T(OWN), *Z(NEAR)) + mul(*T(NEAR), *R(Z_NN)))
     arrive(T_NO)
     add(acc_y, OWN, mul(*Y(NEAR), *R(T_NO)))
-    pass_on(2)
+    pass_on(1, range(2, 3))
     arrive(T_NN)
     add(acc_y, NEAR, mul(*Y(NEAR), *R(T_NN)))
+    put(acc_z, FAR, mul(*T(OWN), *Z(FAR)))
+    put(acc_z, SIDE, mul(*T(OWN), *Z(SIDE)))
+    pass_on(1, range(3, 4))
     arrive(Y_XX)
-    set_factor(FAR, get(acc_z, FAR) + mul(*Z(FAR), *R(Y_XX)))
-    put(acc_z, FAR, mul(*T(OWN), *Z(FAR)))
+    set_factor(FAR, get(acc_p, FAR) + mul(*Z(FAR), *R(Y_XX)))
     put(acc_y, FAR, mul(*Y(OWN), *T(FAR)))
-    arrive(Z_XO)
-    add(acc_z, OWN, mul(*T(FAR), *R(Z_XO)))
+    pass_on(2, range(0, 1))
     arrive(Y_SS)
-    set_factor(SIDE, get(acc_z, SIDE) + mul(*Z(SIDE), *R(Y_SS)))
-    put(acc_z, SIDE, mul(*T(OWN), *Z(SIDE)))
+    set_factor(SIDE, get(acc_p, SIDE) + mul(*Z(SIDE), *R(Y_SS)))
     put(acc_y, SIDE, mul(*Y(OWN), *T(SIDE)))
+    pass_on(2, range(1, PARTS))
+    arrive(Z_XX)
+    add(acc_z, FAR, mul(*T(FAR), *R(Z_XX)))
     arrive(Z_SS)
     add(acc_z, SIDE, mul(*T(SIDE), *R(Z_SS)))
-    arrive(Z_XX)
-    add(acc_z, FAR, mul(*T(FAR), *R(Z_XX)))
-    other = mul(*R(Z_XX), *R(Y_XO)) + mul(*R(Z_XO), *Y(OWN))
+    cross[...] = mul(*R(Z_XX), *R(Y_XO))
+    arrive(T_SS)
+    add(acc_y, SIDE, mul(*Y(SIDE), *R(T_SS)))
+    arrive(T_XX)
+    add(acc_y, FAR, mul(*Y(FAR), *R(T_XX)))
     for s in range(ROWS):
-        for e in range(ROWS):
-            value = (-0.5 * kept_far[s][e]) * other[s * BLK:(s + 1) * BLK, e * BLK:(e + 1) * BLK]
-            h, l = split(value)
-            rh[(Z_XX, *blk(s, e))] = h
-            rl[(Z_XX, *blk(s, e))] = l
-    add(acc_y, OWN, mul(*Y(FAR), *R(Z_XX)))
+        for j in range(s * PARTS // ROWS, (s + 1) * PARTS // ROWS):
+            last_copy(j).wait_recv()
+        rows = pl.ds(s * HALF, HALF)
+        high, low = split(recv[Z_XO, rows])
+        add(acc_z, OWN, mul(th[FAR, :, rows], tl[FAR, :, rows], high, low))
+        value = cross[rows] + mul(high, low, *Y(OWN))
+        value = -0.5 * jnp.concatenate(
+            [kept_far[s][e] * value[:, e * BLK:(e + 1) * BLK] for e in range(ROWS)], axis=1)
+        high, low = split(value)
+        add(acc_y, OWN, mul(yh[FAR, :, rows], yl[FAR, :, rows], high, low))
 
     def emit(result, out):
         for s in range(ROWS):
@@ -280,21 +332,25 @@
                 out[s, :, pl.ds(p * BLK, BLK)] = keep[s][p] * result[place_of[s][p], s]
 
     emit(acc_z, zn_ref)
-    arrive(T_SS)
-    add(acc_y, SIDE, mul(*Y(SIDE), *R(T_SS)))
-    arrive(T_XX)
-    add(acc_y, FAR, mul(*Y(FAR), *R(T_XX)))
     emit(acc_y, yn_ref)
     for copy in copies.values():
         copy.wait_send()
-    for number in range(len(SIDES)):
-        for j in range(RUN):
-            side_copy(own_y.at[OWN], number, j).wait_send()
-
-    @pl.when(place != 0)
+    for j in range(PARTS):
+        last_copy(j).wait_send()
+    for n in range(len(FARS)):
+        for j in range(PARTS):
+            far_copy(own_y.at[OWN], n, j).wait_send()
+            side_copy(own_y.at[OWN], n, j).wait_send()
+
+    @pl.when(head)
     def _():
-        for number in range(len(SIDES)):
-            relay_copy(number).wait_send()
+        for n in range(len(FARS)):
+            for j in range(PARTS):
+                on_far(n, j).wait_send()
+
+    @pl.when(jnp.logical_not(head))
+    def _():
+        on_detour().wait_send()
 
 
 def write_out(y_ref, z_ref, y_hbm, z_hbm, sem):
@@ -318,6 +374,7 @@
     f32 = lambda n: pltpu.VMEM((n, *unit), jnp.float32)
     b16 = lambda n: pltpu.VMEM((n, *unit), jnp.bfloat16)
     hbm = pl.BlockSpec(memory_space=pltpu.HBM)
+    stay = lambda array: pltpu.with_memory_space_constraint(array, pltpu.HBM)
     dma = pltpu.SemaphoreType.DMA
     results = pl.pallas_call(
         functools.partial(kernel, row_count, col_count),
@@ -327,16 +384,16 @@
         scratch_shapes=[
             pltpu.SMEM(pattern.shape[::-1], jnp.int32), pltpu.SMEM(pattern.shape[::-1], jnp.int32),
             pltpu.VMEM(whole.shape, jnp.float32), pltpu.VMEM(whole.shape, jnp.float32),
-            f32(4), f32(4), f32(2), f32(14), pltpu.VMEM((len(SIDES), CHUNK, UNIT), jnp.float32),
+            f32(4), f32(4), f32(2), f32(14), f32(3), pltpu.VMEM((CHUNK, UNIT), jnp.float32), pltpu.VMEM(unit, jnp.float32),
             b16(4), b16(4), b16(4), b16(4), b16(4), b16(4), b16(14), b16(14),
             pltpu.VMEM((SLOTS, ROWS, BLK, BLK), jnp.float32),
             pltpu.VMEM((SLOTS, ROWS, BLK, BLK), jnp.float32),
-            dma((14,)), dma((14,)), dma((len(SIDES), RUN)), dma((len(SIDES), RUN)),
-            dma((len(SIDES),)), dma((len(SIDES),)), dma((4,)),
+            pltpu.VMEM((SLOTS, ROWS, BLK, BLK), jnp.float32),
+            dma((14,)), dma((14,)), *[dma((3, PARTS))] * 6, dma((PARTS,)), dma((PARTS,)), dma((2,)), dma((4,)),
         ],
         compiler_params=pltpu.CompilerParams(
             collective_id=0, has_side_effects=True, vmem_limit_bytes=54_000_000),
-    )(pattern.T, keep_mask.T, sqrt_iterate, inverse_iterate)
+    )(*map(stay, (pattern.T, keep_mask.T, sqrt_iterate, inverse_iterate)))
     return pl.pallas_call(
         write_out,
         out_shape=(whole, whole),

time: 45.5 us -> 43.2 us (0.949); the launches traced: 44.9 us -> 43 us
  local copies, waits for them, and re-layouts: 1.39 us -> 0 us
    unnamed x4 -> x0, local copies, waits for them, and re-layouts: 1.39 us -> none
where the time goes in v3:
time: 43.2 us; the launch traced here: 43 us
  Pallas kernels  42.4 us (98%)
  between operations  0.64 us (1%)
    pallas_call x1, Pallas kernels, local(): pl.pallas_call(functools.partial(kernel, row_count, col_count), out_shape...  41 us
    pallas_call x1, Pallas kernels, local(): pl.pallas_call(write_out, out_shape=(whole, whole), in_specs=[vmem, vmem]...  1.38 us

profile of v3, /device:TPU:0, one launch (start us, length us, event | category | flops | bytes accessed | tf_op | source)
XLA Modules:
  0.0 43.0 jit_solution(10134910091999996954)
XLA Ops:
  0.6 41.0 %shard_map.59 = (f32[2,128,1024]{2,1,0:T(8,128)S(1)}, f32[2,128,1024]{2,1,0:T(8,128)S(1)}) custom-call(s32[8,256]{1,0:T(8,128)} %bitcast.2, s32[8,256]{1,0:T(8,128)} %bitcast.3, f32[2,128,1024]{2,1,0:T(8,128)} %y_hbm.1, f32[2,128,1024]{2,1,0:T(8,128)} %z_hbm.1), custom_call_target="tpu_custom_call" | custom-call | tf_op jit(solution)/shard_map/pallas_call | solution.py:379
  41.7 1.4 %shard_map.60 = (f32[2,128,1024]{2,1,0:T(8,128)}, f32[2,128,1024]{2,1,0:T(8,128)}) custom-call(f32[2,128,1024]{2,1,0:T(8,128)S(1)} %get-tuple-element.4.y_ref, f32[2,128,1024]{2,1,0:T(8,128)S(1)} %get-tuple-element.5.z_ref), custom_call_target="tpu_custom_call" | custom-call | tf_op jit(solution)/shard_map/pallas_call | solution.py:397

commit v4 on v3

--- a/solution.py
+++ b/solution.py
@@ -19,6 +19,8 @@
 PARTS = 4
 CHUNK = UNIT // PARTS
 HALF = UNIT // 2
+CARRY = 40
+assert UNIT - (PARTS - 1) * CARRY >= HALF
 
 (Y_NO, Y_NN, Z_NO, Z_NN, T_NO, T_NN,
  Y_XO, Y_XX, Z_XO, Z_XX, T_XX,
@@ -37,7 +39,7 @@
            pat_ref, keep_ref, y_ref, z_ref,
            own_y, own_z, own_t, recv, relay, bypass, cross, yh, yl, zh, zl, th, tl, rh, rl, acc_y, acc_z, acc_p,
            send_sem, recv_sem, far_send, far_recv, side_send, side_recv, relay_send, relay_recv,
-           last_send, last_recv, bypass_sem, load_sem):
+           last_send, last_recv, bypass_sem, load_sem, ready):
     loads = [
         pltpu.make_async_copy(source, target, load_sem.at[i])
         for i, (source, target) in enumerate((
@@ -50,7 +52,6 @@
     odd = lax.rem(row, 2)
     near = (row + 1 - 2 * odd, col)
     far = (lax.rem(row + row_count - 1 + 2 * odd, row_count), col)
-    side = (row, lax.rem(col + 1, col_count))
     back = (row, lax.rem(col + col_count - 1, col_count))
     place = lax.rem(col, RUN)
     head = place == 0
@@ -61,18 +62,29 @@
     twin_back = (row, lax.rem(twin_col + col_count - 1, col_count))
 
     barrier = pltpu.get_barrier_semaphore()
-    others = [near, twin_far]
-    others += [(row, lax.rem(col + d, col_count)) for d in range(1, col_count)]
-    others += [(far[0], first_col + d) for d in range(RUN)]
-    for other in others:
-        pl.semaphore_signal(barrier, inc=1, device_id=other, device_id_type=MESH)
+    def enter(*targets):
+        for target in targets:
+            pl.semaphore_signal(barrier, inc=1, device_id=target, device_id_type=MESH)
+
+    enter(far, near)
+
+    @pl.when(head)
+    def _():
+        enter(twin, twin_far)
+        for d in range(1, RUN):
+            enter((row, col + d), (far[0], col + d))
+
+    @pl.when(jnp.logical_and(place > 0, place < RUN - 1))
+    def _():
+        enter((row, col + 1))
+
     loads[0].wait()
     loads[1].wait()
 
     def first(place):
         return (place[0] * col_count + place[1]) * ROWS
 
-    starts = [first(place) for place in ((row, col), near, far, side)]
+    starts = [first(place) for place in ((row, col), near, far, (row, lax.rem(col + 1, col_count)))]
     labels = [pat_ref[0, starts[q // ROWS] + q % ROWS] for q in range(SLOTS)]
 
     def pick(wanted, keys, values):
@@ -116,7 +128,11 @@
                     high[where] = h
                     low[where] = l
 
-    pl.semaphore_wait(barrier, len(others))
+    pl.semaphore_wait(barrier, jnp.where(place > 1, 5, 4))
+
+    @pl.when(jnp.logical_not(head))
+    def _():
+        pl.semaphore_signal(ready, inc=1, device_id=(row, first_col), device_id_type=MESH)
 
     copies = {}
 
@@ -171,37 +187,41 @@
                 on_far(n, j).start()
                 on_side(n, j).start()
 
+    def carried(j):
+        return pl.ds(pl.multiple_of(UNIT - (PARTS - j) * CARRY, 8), CARRY)
+
+    def last_rows(j):
+        return carried(j) if j else pl.ds(0, UNIT - (PARTS - 1) * CARRY)
+
     def last_copy(j):
-        return remote(own_z.at[FAR, chunk(j)], recv.at[Z_XO, chunk(j)], last_send.at[j], last_recv.at[j], far)
+        return remote(own_z.at[FAR, last_rows(j)], recv.at[Z_XO, last_rows(j)], last_send.at[j], last_recv.at[j], far)
 
     def detour_copy(j):
-        return remote(own_z.at[FAR, chunk(j)], bypass, last_send.at[j], bypass_sem.at[0], (row, col + j))
+        return remote(own_z.at[FAR, carried(j)], bypass, last_send.at[j], bypass_sem.at[0], (row, col + j))
 
     def on_detour():
-        return remote(bypass, recv.at[Z_XO, chunk(place)], bypass_sem.at[1], last_recv.at[place], (far[0], first_col))
+        return remote(bypass, recv.at[Z_XO, carried(place)], bypass_sem.at[1], last_recv.at[place], (far[0], first_col))
 
     def send_last_direct():
-        last_copy(0).start()
-
         @pl.when(jnp.logical_not(head))
         def _():
-            for j in range(1, PARTS):
+            for j in range(PARTS):
                 last_copy(j).start()
 
     def send_last_detour():
         @pl.when(head)
         def _():
+            pl.semaphore_wait(ready, RUN - 1)
             for j in range(1, PARTS):
                 detour_copy(j).start()
 
     def pass_detour():
         @pl.when(jnp.logical_not(head))
         def _():
-            detour_copy(0).wait_recv()
+            detour_copy(1).wait_recv()
             on_detour().start()
 
     send(own_y.at[FAR], Y_XO, far)
-    send_last_detour()
     send_own(own_y.at[OWN], 0)
     send_own(own_z.at[OWN], 1)
     send(own_y.at[NEAR], Y_NO, near)
@@ -275,10 +295,15 @@
     put(acc_p, FAR, mul(*Z(OWN), *Y(FAR)))
     put(acc_p, SIDE, mul(*Z(OWN), *Y(SIDE)))
     put(acc_y, NEAR, mul(*Y(OWN), *T(NEAR)))
+    send_last_detour()
     pass_detour()
     pass_on(0)
     arrive(Y_XO)
     set_factor(OWN, get(acc_z, OWN) + mul(*Z(FAR), *R(Y_XO)))
+    @pl.when(head)
+    def _():
+        last_copy(0).start()
+
     send_own(own_t.at[OWN], 2)
     send(own_t.at[OWN], T_NN, near)
     send_last_direct()
@@ -315,7 +340,7 @@
     arrive(T_XX)
     add(acc_y, FAR, mul(*Y(FAR), *R(T_XX)))
     for s in range(ROWS):
-        for j in range(s * PARTS // ROWS, (s + 1) * PARTS // ROWS):
+        for j in ((0,), range(1, PARTS))[s]:
             last_copy(j).wait_recv()
         rows = pl.ds(s * HALF, HALF)
         high, low = split(recv[Z_XO, rows])
@@ -384,12 +409,12 @@
         scratch_shapes=[
             pltpu.SMEM(pattern.shape[::-1], jnp.int32), pltpu.SMEM(pattern.shape[::-1], jnp.int32),
             pltpu.VMEM(whole.shape, jnp.float32), pltpu.VMEM(whole.shape, jnp.float32),
-            f32(4), f32(4), f32(2), f32(14), f32(3), pltpu.VMEM((CHUNK, UNIT), jnp.float32), pltpu.VMEM(unit, jnp.float32),
+            f32(4), f32(4), f32(2), f32(14), f32(3), pltpu.VMEM((CARRY, UNIT), jnp.float32), pltpu.VMEM(unit, jnp.float32),
             b16(4), b16(4), b16(4), b16(4), b16(4), b16(4), b16(14), b16(14),
             pltpu.VMEM((SLOTS, ROWS, BLK, BLK), jnp.float32),
             pltpu.VMEM((SLOTS, ROWS, BLK, BLK), jnp.float32),
             pltpu.VMEM((SLOTS, ROWS, BLK, BLK), jnp.float32),
-            dma((14,)), dma((14,)), *[dma((3, PARTS))] * 6, dma((PARTS,)), dma((PARTS,)), dma((2,)), dma((4,)),
+            dma((14,)), dma((14,)), *[dma((3, PARTS))] * 6, dma((PARTS,)), dma((PARTS,)), dma((2,)), dma((4,)), pltpu.SemaphoreType.REGULAR,
         ],
         compiler_params=pltpu.CompilerParams(
             collective_id=0, has_side_effects=True, vmem_limit_bytes=54_000_000),

time: 43.2 us -> 41.2 us (0.954)
  Pallas kernels: 42.4 us -> 40.4 us
    pallas_call x1, Pallas kernels: 41 us -> 39.1 us  [local(): pl.pallas_call(functools.partial(kernel, row_count, col_count), out_shape...]
where the time goes in v4:
time: 41.2 us; the launch traced here: 41.1 us
  Pallas kernels  40.4 us (98%)
  between operations  0.64 us (2%)
    pallas_call x1, Pallas kernels, local(): pl.pallas_call(functools.partial(kernel, row_count, col_count), out_shape...  39.1 us
    pallas_call x1, Pallas kernels, local(): pl.pallas_call(write_out, out_shape=(whole, whole), in_specs=[vmem, vmem]...  1.38 us

profile of v4, /device:TPU:0, one launch (start us, length us, event | category | flops | bytes accessed | tf_op | source)
XLA Modules:
  0.0 41.1 jit_solution(12732951767192448248)
XLA Ops:
  0.6 39.1 %shard_map.59 = (f32[2,128,1024]{2,1,0:T(8,128)S(1)}, f32[2,128,1024]{2,1,0:T(8,128)S(1)}) custom-call(s32[8,256]{1,0:T(8,128)} %bitcast.2, s32[8,256]{1,0:T(8,128)} %bitcast.3, f32[2,128,1024]{2,1,0:T(8,128)} %y_hbm.1, f32[2,128,1024]{2,1,0:T(8,128)} %z_hbm.1), custom_call_target="tpu_custom_call" | custom-call | tf_op jit(solution)/shard_map/pallas_call | solution.py:404
  39.7 1.4 %shard_map.60 = (f32[2,128,1024]{2,1,0:T(8,128)}, f32[2,128,1024]{2,1,0:T(8,128)}) custom-call(f32[2,128,1024]{2,1,0:T(8,128)S(1)} %get-tuple-element.4.y_ref, f32[2,128,1024]{2,1,0:T(8,128)S(1)} %get-tuple-element.5.z_ref), custom_call_target="tpu_custom_call" | custom-call | tf_op jit(solution)/shard_map/pallas_call | solution.py:422

commit v5 on v4

--- a/solution.py
+++ b/solution.py
@@ -112,10 +112,9 @@
     def blk(s, e):
         return pl.ds(s * BLK, BLK), pl.ds(e * BLK, BLK)
 
-    for load, source, whole, high, low in (
-            (loads[2], y_ref, own_y, yh, yl), (loads[3], z_ref, own_z, zh, zl)):
+    def arrange(load, source, whole, high, low):
         load.wait()
-        for g in range(4):
+        for g in (FAR, OWN, NEAR, SIDE):
             for s in range(ROWS):
                 for e in range(ROWS):
                     slot = slot_of[s][g * ROWS + e]
@@ -128,6 +127,7 @@
                     high[where] = h
                     low[where] = l
 
+    arrange(loads[2], y_ref, own_y, yh, yl)
     pl.semaphore_wait(barrier, jnp.where(place > 1, 5, 4))
 
     @pl.when(jnp.logical_not(head))
@@ -223,9 +223,10 @@
 
     send(own_y.at[FAR], Y_XO, far)
     send_own(own_y.at[OWN], 0)
-    send_own(own_z.at[OWN], 1)
     send(own_y.at[NEAR], Y_NO, near)
     send(own_y.at[OWN], Y_NN, near)
+    arrange(loads[3], z_ref, own_z, zh, zl)
+    send_own(own_z.at[OWN], 1)
     send(own_z.at[NEAR], Z_NO, near)
     send(own_z.at[OWN], Z_NN, near)
 

time: 41.2 us -> 40.5 us (0.983)
  Pallas kernels: 40.4 us -> 39.7 us
    pallas_call x1, Pallas kernels: 39.1 us -> 38.3 us  [local(): pl.pallas_call(functools.partial(kernel, row_count, col_count), out_shape...]
where the time goes in v5:
time: 40.5 us; the launch traced here: 40.3 us
  Pallas kernels  39.7 us (98%)
  between operations  0.64 us (2%)
    pallas_call x1, Pallas kernels, local(): pl.pallas_call(functools.partial(kernel, row_count, col_count), out_shape...  38.3 us
    pallas_call x1, Pallas kernels, local(): pl.pallas_call(write_out, out_shape=(whole, whole), in_specs=[vmem, vmem]...  1.38 us

profile of v5, /device:TPU:0, one launch (start us, length us, event | category | flops | bytes accessed | tf_op | source)
XLA Modules:
  0.0 40.3 jit_solution(14872176798649693645)
XLA Ops:
  0.6 38.3 %shard_map.59 = (f32[2,128,1024]{2,1,0:T(8,128)S(1)}, f32[2,128,1024]{2,1,0:T(8,128)S(1)}) custom-call(s32[8,256]{1,0:T(8,128)} %bitcast.2, s32[8,256]{1,0:T(8,128)} %bitcast.3, f32[2,128,1024]{2,1,0:T(8,128)} %y_hbm.1, f32[2,128,1024]{2,1,0:T(8,128)} %z_hbm.1), custom_call_target="tpu_custom_call" | custom-call | tf_op jit(solution)/shard_map/pallas_call | solution.py:405
  39.0 1.4 %shard_map.60 = (f32[2,128,1024]{2,1,0:T(8,128)}, f32[2,128,1024]{2,1,0:T(8,128)}) custom-call(f32[2,128,1024]{2,1,0:T(8,128)S(1)} %get-tuple-element.4.y_ref, f32[2,128,1024]{2,1,0:T(8,128)S(1)} %get-tuple-element.5.z_ref), custom_call_target="tpu_custom_call" | custom-call | tf_op jit(solution)/shard_map/pallas_call | solution.py:423

commit v6 on v5

--- a/solution.py
+++ b/solution.py
@@ -20,7 +20,7 @@
 CHUNK = UNIT // PARTS
 HALF = UNIT // 2
 CARRY = 40
-assert UNIT - (PARTS - 1) * CARRY >= HALF
+assert UNIT - (RUN - 1) * CARRY >= HALF
 
 (Y_NO, Y_NN, Z_NO, Z_NN, T_NO, T_NN,
  Y_XO, Y_XX, Z_XO, Z_XX, T_XX,
@@ -157,6 +157,12 @@
     def side_copy(source, n, j):
         return remote(source.at[chunk(j)], recv.at[SIDES[n], chunk(j)], side_send.at[n, j], side_recv.at[n, j], back)
 
+    def far_whole(source, n):
+        return remote(source, recv.at[FARS[n]], far_send.at[n, 0], far_recv.at[n, 0], far)
+
+    def side_whole(source, n):
+        return remote(source, recv.at[SIDES[n]], side_send.at[n, 0], side_recv.at[n, 0], back)
+
     def twin_copy(source, n, j):
         return remote(source.at[chunk(j)], relay.at[n, chunk(j)], far_send.at[n, j], relay_recv.at[n, j], twin)
 
@@ -174,10 +180,8 @@
 
         @pl.when(jnp.logical_not(head))
         def _():
-            for j in range(PARTS):
-                far_copy(source, n, j).start()
-            for j in range(PARTS):
-                side_copy(source, n, j).start()
+            far_whole(source, n).start()
+            side_whole(source, n).start()
 
     def pass_on(n, chunks=range(PARTS)):
         @pl.when(head)
@@ -188,10 +192,10 @@
                 on_side(n, j).start()
 
     def carried(j):
-        return pl.ds(pl.multiple_of(UNIT - (PARTS - j) * CARRY, 8), CARRY)
+        return pl.ds(pl.multiple_of(UNIT - (RUN - j) * CARRY, 8), CARRY)
 
     def last_rows(j):
-        return carried(j) if j else pl.ds(0, UNIT - (PARTS - 1) * CARRY)
+        return carried(j) if j else pl.ds(0, UNIT - (RUN - 1) * CARRY)
 
     def last_copy(j):
         return remote(own_z.at[FAR, last_rows(j)], recv.at[Z_XO, last_rows(j)], last_send.at[j], last_recv.at[j], far)
@@ -205,14 +209,14 @@
     def send_last_direct():
         @pl.when(jnp.logical_not(head))
         def _():
-            for j in range(PARTS):
+            for j in range(RUN):
                 last_copy(j).start()
 
     def send_last_detour():
         @pl.when(head)
         def _():
             pl.semaphore_wait(ready, RUN - 1)
-            for j in range(1, PARTS):
+            for j in range(1, RUN):
                 detour_copy(j).start()
 
     def pass_detour():
@@ -232,11 +236,23 @@
 
     def arrive(unit):
         if unit in SIDES:
-            for j in range(PARTS):
-                side_copy(own_y.at[OWN], SIDES.index(unit), j).wait_recv()
+            @pl.when(place == RUN - 1)
+            def _():
+                for j in range(PARTS):
+                    side_copy(own_y.at[OWN], SIDES.index(unit), j).wait_recv()
+
+            @pl.when(place != RUN - 1)
+            def _():
+                side_whole(own_y.at[OWN], SIDES.index(unit)).wait_recv()
         elif unit in FARS:
-            for j in range(PARTS):
-                far_copy(own_y.at[OWN], FARS.index(unit), j).wait_recv()
+            @pl.when(head)
+            def _():
+                for j in range(PARTS):
+                    far_copy(own_y.at[OWN], FARS.index(unit), j).wait_recv()
+
+            @pl.when(jnp.logical_not(head))
+            def _():
+                far_whole(own_y.at[OWN], FARS.index(unit)).wait_recv()
         else:
             copies[unit].wait_recv()
         h, l = split(recv[unit])
@@ -341,7 +357,7 @@
     arrive(T_XX)
     add(acc_y, FAR, mul(*Y(FAR), *R(T_XX)))
     for s in range(ROWS):
-        for j in ((0,), range(1, PARTS))[s]:
+        for j in ((0,), range(1, RUN))[s]:
             last_copy(j).wait_recv()
         rows = pl.ds(s * HALF, HALF)
         high, low = split(recv[Z_XO, rows])
@@ -361,21 +377,22 @@
     emit(acc_y, yn_ref)
     for copy in copies.values():
         copy.wait_send()
-    for j in range(PARTS):
+    for j in range(RUN):
         last_copy(j).wait_send()
-    for n in range(len(FARS)):
-        for j in range(PARTS):
-            far_copy(own_y.at[OWN], n, j).wait_send()
-            side_copy(own_y.at[OWN], n, j).wait_send()
 
     @pl.when(head)
     def _():
         for n in range(len(FARS)):
             for j in range(PARTS):
+                twin_copy(own_y.at[OWN], n, j).wait_send()
                 on_far(n, j).wait_send()
+                on_side(n, j).wait_send()
 
     @pl.when(jnp.logical_not(head))
     def _():
+        for n in range(len(FARS)):
+            far_whole(own_y.at[OWN], n).wait_send()
+            side_whole(own_y.at[OWN], n).wait_send()
         on_detour().wait_send()
 
 
@@ -415,7 +432,7 @@
             pltpu.VMEM((SLOTS, ROWS, BLK, BLK), jnp.float32),
             pltpu.VMEM((SLOTS, ROWS, BLK, BLK), jnp.float32),
             pltpu.VMEM((SLOTS, ROWS, BLK, BLK), jnp.float32),
-            dma((14,)), dma((14,)), *[dma((3, PARTS))] * 6, dma((PARTS,)), dma((PARTS,)), dma((2,)), dma((4,)), pltpu.SemaphoreType.REGULAR,
+            dma((14,)), dma((14,)), *[dma((3, PARTS))] * 6, dma((RUN,)), dma((RUN,)), dma((2,)), dma((4,)), pltpu.SemaphoreType.REGULAR,
         ],
         compiler_params=pltpu.CompilerParams(
             collective_id=0, has_side_effects=True, vmem_limit_bytes=54_000_000),

time: 40.5 us -> 40.5 us (level)
  no operation moved by 1% of the time
where the time goes in v6:
time: 40.5 us; the launch traced here: 40.3 us
  Pallas kernels  39.7 us (98%)
  between operations  0.64 us (2%)
    pallas_call x1, Pallas kernels, local(): pl.pallas_call(functools.partial(kernel, row_count, col_count), out_shape...  38.3 us
    pallas_call x1, Pallas kernels, local(): pl.pallas_call(write_out, out_shape=(whole, whole), in_specs=[vmem, vmem]...  1.38 us

profile of v6, /device:TPU:0, one launch (start us, length us, event | category | flops | bytes accessed | tf_op | source)
XLA Modules:
  0.0 40.3 jit_solution(13564098251176679832)
XLA Ops:
  0.6 38.3 %shard_map.59 = (f32[2,128,1024]{2,1,0:T(8,128)S(1)}, f32[2,128,1024]{2,1,0:T(8,128)S(1)}) custom-call(s32[8,256]{1,0:T(8,128)} %bitcast.2, s32[8,256]{1,0:T(8,128)} %bitcast.3, f32[2,128,1024]{2,1,0:T(8,128)} %y_hbm.1, f32[2,128,1024]{2,1,0:T(8,128)} %z_hbm.1), custom_call_target="tpu_custom_call" | custom-call | tf_op jit(solution)/shard_map/pallas_call | solution.py:422
  39.0 1.4 %shard_map.60 = (f32[2,128,1024]{2,1,0:T(8,128)}, f32[2,128,1024]{2,1,0:T(8,128)}) custom-call(f32[2,128,1024]{2,1,0:T(8,128)S(1)} %get-tuple-element.4.y_ref, f32[2,128,1024]{2,1,0:T(8,128)S(1)} %get-tuple-element.5.z_ref), custom_call_target="tpu_custom_call" | custom-call | tf_op jit(solution)/shard_map/pallas_call | solution.py:440

commit v7 on v6

--- a/solution.py
+++ b/solution.py
@@ -45,8 +45,6 @@
         for i, (source, target) in enumerate((
             (pat_hbm, pat_ref), (keep_hbm, keep_ref), (y_hbm, y_ref), (z_hbm, z_ref)))
     ]
-    for load in loads:
-        load.start()
     row = lax.axis_index("row")
     col = lax.axis_index("col")
     odd = lax.rem(row, 2)
@@ -78,6 +76,8 @@
     def _():
         enter((row, col + 1))
 
+    for load in loads:
+        load.start()
     loads[0].wait()
     loads[1].wait()
 
@@ -400,9 +400,7 @@
     copies = []
     for source, target in ((y_ref, y_hbm), (z_ref, z_hbm)):
         for s in range(ROWS):
-            for part in range(2):
-                where = (s, pl.ds(part * (BLK // 2), BLK // 2))
-                copies.append(pltpu.make_async_copy(source.at[where], target.at[where], sem.at[len(copies)]))
+            copies.append(pltpu.make_async_copy(source.at[s], target.at[s], sem.at[len(copies)]))
     for copy in copies:
         copy.start()
     for copy in copies:
@@ -442,7 +440,7 @@
         out_shape=(whole, whole),
         in_specs=[vmem, vmem],
         out_specs=(hbm, hbm),
-        scratch_shapes=[dma((8,))],
+        scratch_shapes=[dma((4,))],
         compiler_params=pltpu.CompilerParams(vmem_limit_bytes=4194304),
     )(*results)
 

time: 40.5 us -> 40.5 us (level)
  no operation moved by 1% of the time
where the time goes in v7:
time: 40.5 us; the launch traced here: 40.4 us
  Pallas kernels  39.8 us (98%)
  between operations  0.64 us (2%)
    pallas_call x1, Pallas kernels, local(): pl.pallas_call(functools.partial(kernel, row_count, col_count), out_shape...  38.4 us
    pallas_call x1, Pallas kernels, local(): pl.pallas_call(write_out, out_shape=(whole, whole), in_specs=[vmem, vmem]...  1.35 us

profile of v7, /device:TPU:0, one launch (start us, length us, event | category | flops | bytes accessed | tf_op | source)
XLA Modules:
  0.0 40.4 jit_solution(15083412293951828675)
XLA Ops:
  0.6 38.4 %shard_map.59 = (f32[2,128,1024]{2,1,0:T(8,128)S(1)}, f32[2,128,1024]{2,1,0:T(8,128)S(1)}) custom-call(s32[8,256]{1,0:T(8,128)} %bitcast.2, s32[8,256]{1,0:T(8,128)} %bitcast.3, f32[2,128,1024]{2,1,0:T(8,128)} %y_hbm.1, f32[2,128,1024]{2,1,0:T(8,128)} %z_hbm.1), custom_call_target="tpu_custom_call" | custom-call | tf_op jit(solution)/shard_map/pallas_call | solution.py:420
  39.1 1.3 %shard_map.60 = (f32[2,128,1024]{2,1,0:T(8,128)}, f32[2,128,1024]{2,1,0:T(8,128)}) custom-call(f32[2,128,1024]{2,1,0:T(8,128)S(1)} %get-tuple-element.4.y_ref, f32[2,128,1024]{2,1,0:T(8,128)S(1)} %get-tuple-element.5.z_ref), custom_call_target="tpu_custom_call" | custom-call | tf_op jit(solution)/shard_map/pallas_call | solution.py:438
